TPU v7x, 8 devices: a whole 2x2x1 slice. The times are simulated.
8 devices in a mesh: dp: 2 (over z, y), tp: 4 (over x, core).
Axes of the slice: x: 2, y: 2, z: 1, core: 2. Of those that a mesh axis runs over, the one named last changes fastest.
Arguments:
- hidden: bfloat16 [2, 1024, 2048], P('dp', 'tp'), parts along dimension 0
- grad_out: bfloat16 [2, 1024, 2048], P('dp', 'tp'), parts along dimension 0
- ln1_gain: bfloat16 [2048], replicated
- ln1_bias: bfloat16 [2048], replicated
- w_qkv: bfloat16 [2048, 3, 32, 64], P(None, None, 'tp')
- b_qkv: bfloat16 [3, 32, 64], P(None, 'tp')
- w_out: bfloat16 [32, 64, 2048], P('tp')
- b_out: bfloat16 [2048], replicated
- ln2_gain: bfloat16 [2048], replicated
- ln2_bias: bfloat16 [2048], replicated
- w_up: bfloat16 [2048, 8192], P(None, 'tp')
- b_up: bfloat16 [8192], P('tp')
- w_down: bfloat16 [8192, 2048], P('tp')
- b_down: bfloat16 [2048], replicated
Outputs:
- output 1: bfloat16 [2, 1024, 2048], P('dp', 'tp'), parts along dimension 0
- output 2: bfloat16 [2, 1024, 2048], P('dp', 'tp'), parts along dimension 0
- output 3: float32 [4096], P('dp'), parts along dimension 0
- output 4: float32 [4096], P('dp'), parts along dimension 0
- output 5: float32 [4096, 3, 32, 64], P('dp', None, 'tp'), parts along dimension 0
- output 6: float32 [6, 32, 64], P('dp', 'tp'), parts along dimension 0
- output 7: float32 [64, 64, 2048], P(('dp', 'tp')), parts along dimension 0
- output 8: float32 [4096], P('dp'), parts along dimension 0
- output 9: float32 [4096], P('dp'), parts along dimension 0
- output 10: float32 [4096], P('dp'), parts along dimension 0
- output 11: float32 [4096, 8192], P('dp', 'tp'), parts along dimension 0
- output 12: float32 [16384], P(('dp', 'tp')), parts along dimension 0
- output 13: float32 [16384, 2048], P(('dp', 'tp')), parts along dimension 0
- output 14: float32 [4096], P('dp'), parts along dimension 0
There are 2 independent parts. A program takes and returns all parts, laid end to end along the dimension named above; an argument that names none is the same for every part.
All inputs are finite; a program needn't handle non-finite values.
Results may differ from a plain program's by a relative error of at most 0.0181765.
Values are sent between devices in bfloat16 or wider.
A program may use at most 1 GiB of HBM per device.

v0:
```python
import jax
import jax.numpy as jnp
from jax import lax
from jax.sharding import PartitionSpec as P

LN_EPS = 1e-5


def norm_forward(value, gain, shift):
    val32 = value.astype(jnp.float32)
    centered = val32 - jnp.mean(val32, axis=-1, keepdims=True)
    inv_std = lax.rsqrt(jnp.mean(centered * centered, axis=-1, keepdims=True) + LN_EPS)
    x_hat = centered * inv_std
    normed = x_hat * gain.astype(jnp.float32) + shift.astype(jnp.float32)
    return normed.astype(jnp.bfloat16), x_hat, inv_std


def norm_backward(grad_normed, x_hat, inv_std, gain):
    grad32 = grad_normed.astype(jnp.float32)
    grad_gain = jnp.sum(grad32 * x_hat, axis=(0, 1))
    grad_shift = jnp.sum(grad32, axis=(0, 1))
    value_a9 = grad32 * gain.astype(jnp.float32)
    grad_input = inv_std * (value_a9 - jnp.mean(value_a9, axis=-1, keepdims=True) - x_hat * jnp.mean(value_a9 * x_hat, axis=-1, keepdims=True))
    return grad_input, grad_gain, grad_shift


def gelu_tanh(value):
    return jax.nn.gelu(value, approximate=True)


def attention_forward(qkv_proj, attn_scale):
    seq_len = qkv_proj.shape[2]
    scores = jnp.einsum("bqhe,bkhe->bhqk", qkv_proj[0], qkv_proj[1], preferred_element_type=jnp.float32) * attn_scale
    positions = jnp.arange(seq_len)
    causal = positions[:, None] >= positions[None, :]
    probs32 = jax.nn.softmax(jnp.where(causal, scores, -1e30), axis=-1)
    probs_bf = probs32.astype(jnp.bfloat16)
    context = jnp.einsum("bhqk,bkhe->bqhe", probs_bf, qkv_proj[2], preferred_element_type=jnp.float32).astype(jnp.bfloat16)
    return context, probs32, probs_bf


def attention_backward(grad_context, qkv_proj, probs32, probs_bf, attn_scale):
    grad_probs = jnp.einsum("bqhe,bkhe->bhqk", grad_context, qkv_proj[2], preferred_element_type=jnp.float32).astype(jnp.bfloat16).astype(jnp.float32)
    row_dot = jnp.sum(grad_probs * probs32, axis=-1, keepdims=True)
    grad_scores = (probs32 * (grad_probs - row_dot) * attn_scale).astype(jnp.bfloat16)
    grad_query = jnp.einsum("bhqk,bkhe->bqhe", grad_scores, qkv_proj[1], preferred_element_type=jnp.float32)
    grad_key = jnp.einsum("bhqk,bqhe->bkhe", grad_scores, qkv_proj[0], preferred_element_type=jnp.float32)
    grad_value = jnp.einsum("bhqk,bqhe->bkhe", probs_bf, grad_context, preferred_element_type=jnp.float32)
    return jnp.stack([grad_query.astype(jnp.bfloat16), grad_key.astype(jnp.bfloat16), grad_value.astype(jnp.bfloat16)])


def solution(mesh):
    def device_step(hidden, grad_out, ln1_gain, ln1_bias, w_qkv, b_qkv, w_out, b_out, ln2_gain, ln2_bias, w_up, b_up, w_down, b_down):
        attn_scale = w_qkv.shape[-1] ** -0.5
        normed1, x_hat1, inv_std1 = norm_forward(hidden, ln1_gain, ln1_bias)
        normed1_all = lax.all_gather(normed1, "tp", axis=1, tiled=True)
        qkv_proj = (jnp.einsum("bsd,dche->cbshe", normed1_all, w_qkv, preferred_element_type=jnp.float32) + b_qkv.astype(jnp.float32)[:, None, None]).astype(jnp.bfloat16)
        context, probs32, probs_bf = attention_forward(qkv_proj, attn_scale)
        attn_part = jnp.einsum("crif,ife->cre", context, w_out, preferred_element_type=jnp.float32).astype(jnp.bfloat16)
        attn_local = lax.psum_scatter(attn_part, "tp", scatter_dimension=1, tiled=True)
        resid1 = (hidden.astype(jnp.float32) + attn_local.astype(jnp.float32) + b_out.astype(jnp.float32)).astype(jnp.bfloat16)
        normed2, x_hat2, inv_std2 = norm_forward(resid1, ln2_gain, ln2_bias)
        normed2_all = lax.all_gather(normed2, "tp", axis=1, tiled=True)
        pre_act = (jnp.einsum("bsd,df->bsf", normed2_all, w_up, preferred_element_type=jnp.float32) + b_up.astype(jnp.float32)).astype(jnp.bfloat16)
        gelu_val, gelu_pull = jax.vjp(gelu_tanh, pre_act.astype(jnp.float32))
        gelu_out = gelu_val.astype(jnp.bfloat16)
        mlp_part = jnp.einsum("bsf,fd->bsd", gelu_out, w_down, preferred_element_type=jnp.float32).astype(jnp.bfloat16)
        mlp_local = lax.psum_scatter(mlp_part, "tp", scatter_dimension=1, tiled=True)
        layer_out = (resid1.astype(jnp.float32) + mlp_local.astype(jnp.float32) + b_down.astype(jnp.float32)).astype(jnp.bfloat16)

        grad_out_all = lax.all_gather(grad_out, "tp", axis=1, tiled=True)
        grad_b_down = jnp.sum(grad_out, axis=(0, 1), dtype=jnp.float32)
        grad_gelu = jnp.einsum("bsd,fd->bsf", grad_out_all, w_down, preferred_element_type=jnp.float32).astype(jnp.bfloat16)
        grad_w_down = jnp.einsum("bsf,bsd->fd", gelu_out, grad_out_all, preferred_element_type=jnp.float32)
        grad_pre = gelu_pull(grad_gelu.astype(jnp.float32))[0].astype(jnp.bfloat16)
        grad_b_up = jnp.sum(grad_pre, axis=(0, 1), dtype=jnp.float32)
        grad_w_up = jnp.einsum("bsd,bsf->df", normed2_all, grad_pre, preferred_element_type=jnp.float32)
        grad_norm2_part = jnp.einsum("bsf,df->bsd", grad_pre, w_up, preferred_element_type=jnp.float32).astype(jnp.bfloat16)
        grad_norm2 = lax.psum_scatter(grad_norm2_part, "tp", scatter_dimension=1, tiled=True)
        grad_resid_ln, grad_ln2_gain, grad_ln2_bias = norm_backward(grad_norm2, x_hat2, inv_std2, ln2_gain)
        grad_resid1 = (grad_out.astype(jnp.float32) + grad_resid_ln).astype(jnp.bfloat16)
        grad_b_out = jnp.sum(grad_resid1, axis=(0, 1), dtype=jnp.float32)
        grad_resid1_all = lax.all_gather(grad_resid1, "tp", axis=1, tiled=True)
        grad_context = jnp.einsum("cre,ife->crif", grad_resid1_all, w_out, preferred_element_type=jnp.float32).astype(jnp.bfloat16)
        grad_w_out = jnp.einsum("crif,cre->ife", context, grad_resid1_all, preferred_element_type=jnp.float32)
        grad_qkv = attention_backward(grad_context, qkv_proj, probs32, probs_bf, attn_scale)
        grad_b_qkv = jnp.sum(grad_qkv, axis=(1, 2), dtype=jnp.float32)
        grad_w_qkv = jnp.einsum("bsd,cbshe->dche", normed1_all, grad_qkv, preferred_element_type=jnp.float32)
        grad_norm1_part = jnp.einsum("cbshe,dche->bsd", grad_qkv, w_qkv, preferred_element_type=jnp.float32).astype(jnp.bfloat16)
        grad_norm1 = lax.psum_scatter(grad_norm1_part, "tp", scatter_dimension=1, tiled=True)
        grad_input_ln, grad_ln1_gain, grad_ln1_bias = norm_backward(grad_norm1, x_hat1, inv_std1, ln1_gain)
        grad_hidden = (grad_resid1.astype(jnp.float32) + grad_input_ln).astype(jnp.bfloat16)
        vec_sums = lax.psum(jnp.stack([grad_ln1_gain, grad_ln1_bias, grad_b_out, grad_ln2_gain, grad_ln2_bias, grad_b_down]), "tp")
        return (layer_out, grad_hidden, vec_sums[0], vec_sums[1], grad_w_qkv, grad_b_qkv, grad_w_out, vec_sums[2], vec_sums[3], vec_sums[4], grad_w_up, grad_b_up, grad_w_down, vec_sums[5])

    act_spec = P("dp", "tp", None)
    vec_spec = P(None)
    group_vec = P("dp")
    in_specs = (act_spec, act_spec, vec_spec, vec_spec, P(None, None, "tp", None), P(None, "tp", None), P("tp", None, None), vec_spec, vec_spec, vec_spec, P(None, "tp"), P("tp"), P("tp", None), vec_spec)
    out_specs = (act_spec, act_spec, group_vec, group_vec, P("dp", None, "tp", None), P("dp", "tp", None), P(("dp", "tp"), None, None), group_vec, group_vec, group_vec, P("dp", "tp"), P(("dp", "tp")), P(("dp", "tp"), None), group_vec)
    return jax.shard_map(device_step, mesh=mesh, in_specs=in_specs, out_specs=out_specs, check_vma=False)
```

profile of v0, /device:TPU:0, one launch (start us, length us, event | category | flops | bytes accessed | tf_op | source)
XLA Modules:
  0.0 532.7 jit_solution(13087128795384931531)
XLA Ops:
  12.5 2.7 fusion.73
  15.5 34.1 %all-gather.5.cloned.1.call-done = bf16[1,1024,2048]{2,1,0:T(8,128)(2,1)} async-done(((bf16[1,256,2048]{2,1,0:T(8,128)(2,1)}), bf16[1,1024,2048]{2,1,0:T(8,128)(2,1)}) %all-gather.5.cloned.1.call-update) | async-done | bytes 4194320 | tf_op jit(solution)/shard_map/all_gather | solution.py:56
  49.6 10.1 %fusion.39 = f32[1024,1536]{0,1:S(1)} fusion(bf16[2048,1536]{0,1:T(8,128)(2,1)} %bitcast.156, bf16[1,1024,2048]{2,1,0:T(8,128)(2,1)} %all-gather.5.cloned.1.call-done), kind=kOutput, calls=%fused_computation.57 | convolution fusion | flops 6442450944 | bytes 16777216
  59.7 2.1 fusion.49
  61.8 19.1 %fusion.118 = (f32[8,1024]{1,0:T(8,128)S(1)}, f32[8,1024,1024]{1,2,0:T(8,128)}) fusion(pred[1024,1024]{0,1:T(8,128)(4,1)S(1)} %iota_compare_fusion, bf16[3,1,1024,8,64]{2,4,3,0,1:T(8,128)(2,1)} %fusion.49), kind=kOutput, calls=%fused_computation.148 | convolution fusion | flops 1107297280 | bytes 36732928 | tf_op jit(solution)/shard_map/sub | solution.py:36
  80.9 12.7 %fusion.101 = bf16[1024,8,64]{0,2,1:T(8,128)(2,1)S(1)} fusion(bf16[3,1,1024,8,64]{2,4,3,0,1:T(8,128)(2,1)} %fusion.49, f32[8,1024,1024]{1,2,0:T(8,128)} %get-tuple-element.37, f32[8,1024]{1,0:T(8,128)S(1)} %get-tuple-element.36), kind=kOutput, calls=%fused_computation.126 | convolution fusion | flops 1091043328 | bytes 35684352 | tf_op jit(solution)/shard_map/bhqk,bkhe->bqhe/dot_general | solution.py:38
  94.6 4.4 fusion.47
  99.7 37.7 %reduce-scatter.5.cloned.1.call-done = bf16[1,256,2048]{2,1,0:T(8,128)(2,1)} async-done(((bf16[1,1024,2048]{2,1,0:T(8,128)(2,1)}), bf16[1,256,2048]{2,1,0:T(8,128)(2,1)}) %reduce-scatter.5.cloned.1.call-update) | async-done | bytes 1048592 | tf_op jit(solution)/shard_map/reduce_scatter | solution.py:60
  142.2 31.0 %all-gather.7.cloned.1.call-done = bf16[1,1024,2048]{2,1,0:T(8,128)(2,1)} async-done(((bf16[1,256,2048]{2,1,0:T(8,128)(2,1)}), bf16[1,1024,2048]{2,1,0:T(8,128)(2,1)}) %all-gather.7.cloned.1.call-update) | async-done | bytes 4194320 | tf_op jit(solution)/shard_map/all_gather | solution.py:63
  173.3 13.8 %add_convert_fusion = bf16[1024,2048]{1,0:T(8,128)(2,1)} fusion(f32[2048]{0:T(1024)S(1)} %convert_element_type.217, bf16[2048,2048]{1,0:T(8,128)(2,1)} %param.24, bf16[1,1024,2048]{2,1,0:T(8,128)(2,1)} %all-gather.7.cloned.1.call-done), kind=kOutput, calls=%fused_computation.36 | convolution fusion | flops 8594128896 | bytes 16785408 | tf_op jit(solution)/shard_map/bsd,df->bsf/dot_general | solution.py:64
  187.1 19.1 %all-gather.9.cloned.1.call-done = bf16[1,1024,2048]{2,1,0:T(8,128)(2,1)} async-done(((bf16[1,256,2048]{2,1,0:T(8,128)(2,1)}), bf16[1,1024,2048]{2,1,0:T(8,128)(2,1)}) %all-gather.9.cloned.1.call-update) | async-done | bytes 4194320 | tf_op jit(solution)/shard_map/all_gather | solution.py:71
  206.2 18.6 %convert_reduce_fusion = (f32[2048]{0:T(1024)}, bf16[1024,2048]{1,0:T(8,128)(2,1)S(1)}) fusion(bf16[1024,2048]{1,0:T(8,128)(2,1)} %add_convert_fusion, bf16[2048,2048]{1,0:T(8,128)(2,1)} %param.26, bf16[1,1024,2048]{2,1,0:T(8,128)(2,1)} %all-gather.9.cloned.1.call-done), kind=kOutput, calls=%fused_computation.35 | convolution fusion | flops 8642361344 | bytes 20979712 | tf_op jit(solution)/shard_map/bsd,fd->bsf/dot_general | solution.py:73
  226.8 13.0 %convert_bitcast_fusion = bf16[1,1024,2048]{2,1,0:T(8,128)(2,1)} fusion(bf16[1024,2048]{1,0:T(8,128)(2,1)S(1)} %get-tuple-element.39, bf16[2048,2048]{1,0:T(8,128)(2,1)} %param.24), kind=kOutput, calls=%fused_computation.59 | convolution fusion | flops 8592031744 | bytes 16777216 | tf_op jit(solution)/shard_map/bsf,df->bsd/dot_general | solution.py:78
  239.9 15.5 %convert_bitcast_fusion.1 = bf16[1,1024,2048]{2,1,0:T(8,128)(2,1)} fusion(bf16[2048,2048]{1,0:T(8,128)(2,1)} %param.26, bf16[1024,2048]{1,0:T(8,128)(2,1)} %add_convert_fusion), kind=kOutput, calls=%fused_computation.60 | convolution fusion | flops 8613003264 | bytes 16777216 | tf_op jit(solution)/shard_map/bsf,fd->bsd/dot_general | solution.py:67
  256.0 22.2 %reduce-scatter.9.cloned.1.call-done = bf16[1,256,2048]{2,1,0:T(8,128)(2,1)} async-done(((bf16[1,1024,2048]{2,1,0:T(8,128)(2,1)}), bf16[1,256,2048]{2,1,0:T(8,128)(2,1)}) %reduce-scatter.9.cloned.1.call-update) | async-done | bytes 1048592 | tf_op jit(solution)/shard_map/reduce_scatter | solution.py:79
  278.3 2.9 fusion.85
  281.2 38.3 %reduce-scatter.7.cloned.1.call-done = bf16[1,256,2048]{2,1,0:T(8,128)(2,1)} async-done(((bf16[1,1024,2048]{2,1,0:T(8,128)(2,1)}), bf16[1,256,2048]{2,1,0:T(8,128)(2,1)}) %reduce-scatter.7.cloned.1.call-update) | async-done | bytes 1048592 | tf_op jit(solution)/shard_map/reduce_scatter | solution.py:68
  319.5 5.5 %convert_reduce_fusion.6 = (f32[2048]{0:T(1024)}, bf16[1,256,2048]{2,1,0:T(8,128)(2,1)}, f32[2048]{0:T(1024)}, bf16[1,256,2048]{2,1,0:T(8,128)(2,1)}) fusion(f32[256]{0:T(256)S(1)} %get-tuple-element.40, f32[256]{0:T(256)S(1)} %broadcast_multiply_fusion.4, bf16[1,256,2048]{2,1,0:T(8,128)(2,1)S(1)} %copy-done.5, f32[256]{0:T(256)S(1)} %get-tuple-element.41, ...), kind=kLoop, calls=%fused_computation.86 | loop fusion | flops 9957376 | bytes 6328320 | tf_op jit(solution)/shard_map/reduce_sum | solution.py:82
  325.2 31.4 %all-gather.11.cloned.1.call-done = bf16[1,1024,2048]{2,1,0:T(8,128)(2,1)} async-done(((bf16[1,256,2048]{2,1,0:T(8,128)(2,1)}), bf16[1,1024,2048]{2,1,0:T(8,128)(2,1)}) %all-gather.11.cloned.1.call-update) | async-done | bytes 4194320 | tf_op jit(solution)/shard_map/all_gather | solution.py:83
  356.7 4.5 fusion.95
  361.2 13.3 %fusion.98 = bf16[1,1,1024,8,64]{2,4,3,1,0:T(8,128)(2,1)S(1)} fusion(bf16[1024,8,64]{0,2,1:T(8,128)(2,1)S(1)} %fusion.95, f32[8,1024,1024]{1,2,0:T(8,128)} %get-tuple-element.37, f32[8,1024]{1,0:T(8,128)S(1)} %get-tuple-element.36), kind=kOutput, calls=%fused_computation.125 | convolution fusion | flops 1091043328 | bytes 35684352 | tf_op jit(solution)/shard_map/bhqk,bqhe->bkhe/dot_general | solution.py:48
  374.6 9.8 %convolution_convert_fusion = bf16[8,1024,1024]{1,2,0:T(8,128)(2,1)} fusion(bf16[1024,8,64]{0,2,1:T(8,128)(2,1)S(1)} %fusion.95, bf16[3,1,1024,8,64]{2,4,3,0,1:T(8,128)(2,1)} %fusion.49), kind=kOutput, calls=%fused_computation.22 | convolution fusion | flops 1082130432 | bytes 18874368 | tf_op jit(solution)/shard_map/bqhe,bkhe->bhqk/dot_general | solution.py:43
  384.4 33.7 %fusion.104 = bf16[1,1,1024,8,64]{2,4,3,1,0:T(8,128)(2,1)S(1)} fusion(bf16[8,1024,1024]{1,2,0:T(8,128)(2,1)} %convolution_convert_fusion, bf16[3,1,1024,8,64]{2,4,3,0,1:T(8,128)(2,1)} %fusion.49, f32[8,1024,1024]{1,2,0:T(8,128)} %get-tuple-element.37, f32[8,1024]{1,0:T(8,128)S(1)} %get-tuple-element.36), kind=kOutput, calls=%fused_computation.127 | convolution fusion | flops 1149772800 | bytes 102825984 | tf_op jit(solution)/shard_map/bhqk,bqhe->bkhe/dot_general | solution.py:47
  418.0 33.4 %fusion.105 = bf16[1,1,1024,8,64]{2,4,3,1,0:T(8,128)(2,1)S(1)} fusion(bf16[8,1024,1024]{1,2,0:T(8,128)(2,1)} %convolution_convert_fusion, bf16[3,1,1024,8,64]{2,4,3,0,1:T(8,128)(2,1)} %fusion.49, f32[8,1024,1024]{1,2,0:T(8,128)} %get-tuple-element.37, f32[8,1024]{1,0:T(8,128)S(1)} %get-tuple-element.36), kind=kOutput, calls=%fused_computation.128 | convolution fusion | flops 1149772800 | bytes 102825984 | tf_op jit(solution)/shard_map/bhqk,bkhe->bqhe/dot_general | solution.py:46
  454.4 11.4 %fusion.48 = bf16[1,1024,2048]{2,1,0:T(8,128)(2,1)} fusion(bf16[2048,3,8,64]{0,3,2,1:T(8,128)(2,1)} %param.18, bf16[3,1,1024,8,64]{2,4,3,1,0:T(8,128)(2,1)S(1)} %get-tuple-element.23), kind=kOutput, calls=%fused_computation.64 | convolution fusion | flops 6444548096 | bytes 13631488 | tf_op jit(solution)/shard_map/cbshe,dche->bsd/dot_general | solution.py:89
  465.8 15.6 %fusion.33 = f32[2048,2048]{1,0:T(8,128)} fusion(bf16[1024,2048]{1,0:T(8,128)(2,1)} %copy-done.29, bf16[1,1024,2048]{2,1,0:T(8,128)(2,1)} %all-gather.7.cloned.1.call-done), kind=kOutput, calls=%fused_computation.51 | convolution fusion | flops 8589934592 | bytes 25165824 | tf_op jit(solution)/shard_map/bsd,bsf->df/dot_general | solution.py:77
  481.4 12.7 %fusion.29 = f32[2048,2048]{1,0:T(8,128)} fusion(bf16[1,1024,2048]{2,1,0:T(8,128)(2,1)S(1)} %copy-done.25, bf16[1024,2048]{1,0:T(8,128)(2,1)S(1)} %copy-done.30), kind=kOutput, calls=%fused_computation.47 | convolution fusion | flops 8610906112 | bytes 25165824 | tf_op jit(solution)/shard_map/bsf,bsd->fd/dot_general | solution.py:74
  494.1 4.4 fusion.25
  498.6 9.4 %fusion.37 = f32[2048,1536]{0,1} fusion(bf16[1024,1536]{0,1:T(8,128)(2,1)S(1)} %bitcast.143, bf16[1,1024,2048]{2,1,0:T(8,128)(2,1)S(1)} %copy-done.24), kind=kOutput, calls=%fused_computation.55 | convolution fusion | flops 6442450944 | bytes 19922944
  508.0 2.3 fusion.86
  510.5 10.8 %psum.7 = f32[6,2048]{1,0:T(8,128)S(1)} all-reduce(f32[6,2048]{1,0:T(8,128)S(1)} %stack.43), channel_id=1, replica_groups=mesh['dp'=2,'tp'=4] {'tp'}, use_global_device_ids=true, to_apply=%region_21.22 | all-reduce | flops 12288 | bytes 98304 | tf_op jit(solution)/shard_map/psum | solution.py:93
  522.0 3.4 fusion.78
  (103 shorter events, 18.6 us)
Async XLA Ops:
  7.2 87.4 %copy-start = (bf16[8,64,2048]{2,1,0:T(8,128)(2,1)S(1)}, bf16[8,64,2048]{2,1,0:T(8,128)(2,1)}, u32[]{:S(2)}) copy-start(bf16[8,64,2048]{2,1,0:T(8,128)(2,1)} %param.20) | copy-start | bytes 6291460
  7.2 8.0 %copy-start.18 = (bf16[3,8,64]{2,1,0:T(8,128)(2,1)S(1)}, bf16[3,8,64]{2,1,0:T(8,128)(2,1)}, u32[]{:S(2)}) copy-start(bf16[3,8,64]{2,1,0:T(8,128)(2,1)} %param.19) | copy-start | bytes 9220
  7.2 42.4 %all-gather.5.cloned.1.call-start = ((), (), s32[]{:S(2)}) async-start(), calls=%async_computation.4 | async-start | bytes 5242880 | tf_op jit(solution)/shard_map/all_gather | solution.py:56
  8.8 3.1 copy-start.8
  10.2 1.7 copy-start.14
  15.2 122.3 %reduce-scatter.5.cloned.1.call-start = ((), (), s32[]{:S(2)}) async-start(), calls=%async_computation.5 | async-start | bytes 5242880 | tf_op jit(solution)/shard_map/reduce_scatter | solution.py:60
  99.0 38.4 %copy-start.2 = (bf16[1,256,2048]{2,1,0:T(8,128)(2,1)S(1)}, bf16[1,256,2048]{2,1,0:T(8,128)(2,1)}, u32[]{:S(2)}) copy-start(bf16[1,256,2048]{2,1,0:T(8,128)(2,1)} %param.14) | copy-start | bytes 3145732
  99.0 74.2 %all-gather.7.cloned.1.call-start = ((), (), s32[]{:S(2)}) async-start(), calls=%async_computation.6 | async-start | bytes 5242880 | tf_op jit(solution)/shard_map/all_gather | solution.py:63
  99.7 42.5 %copy-start.22 = (bf16[2048]{0:T(1024)(128)(2,1)S(1)}, bf16[2048]{0:T(1024)(128)(2,1)}, u32[]{:S(2)}) copy-start(bf16[2048]{0:T(1024)(128)(2,1)} %param.25) | copy-start | bytes 12292
  141.6 64.6 %all-gather.9.cloned.1.call-start = ((), (), s32[]{:S(2)}) async-start(), calls=%async_computation.8 | async-start | bytes 5242880 | tf_op jit(solution)/shard_map/all_gather | solution.py:71
  142.2 136.1 %reduce-scatter.9.cloned.1.call-start = ((), (), s32[]{:S(2)}) async-start(), calls=%async_computation.9 | async-start | bytes 5242880 | tf_op jit(solution)/shard_map/reduce_scatter | solution.py:79
  224.8 1.9 copy-start.29
  239.8 79.7 %reduce-scatter.7.cloned.1.call-start = ((), (), s32[]{:S(2)}) async-start(), calls=%async_computation.7 | async-start | bytes 5242880 | tf_op jit(solution)/shard_map/reduce_scatter | solution.py:68
  255.4 22.9 %copy-start.5 = (bf16[1,256,2048]{2,1,0:T(8,128)(2,1)S(1)}, bf16[1,256,2048]{2,1,0:T(8,128)(2,1)}, u32[]{:S(2)}) copy-start(bf16[1,256,2048]{2,1,0:T(8,128)(2,1)} %copy-done.4) | copy-start | bytes 3145732
  255.4 101.3 %all-gather.11.cloned.1.call-start = ((), (), s32[]{:S(2)}) async-start(), calls=%async_computation.10 | async-start | bytes 5242880 | tf_op jit(solution)/shard_map/all_gather | solution.py:83
  325.0 183.0 %reduce-scatter.11.cloned.1.call-start = ((), (), s32[]{:S(2)}) async-start(), calls=%async_computation.11 | async-start | bytes 5242880 | tf_op jit(solution)/shard_map/reduce_scatter | solution.py:90
  452.7 1.7 copy-start.6
  465.8 15.6 %copy-start.25 = (bf16[1,1024,2048]{2,1,0:T(8,128)(2,1)S(1)}, bf16[1,1024,2048]{2,1,0:T(8,128)(2,1)}, u32[]{:S(2)}) copy-start(bf16[1,1024,2048]{2,1,0:T(8,128)(2,1)} %all-gather.9.cloned.1.call-done) | copy-start | bytes 12582916
  465.8 15.6 %copy-start.30 = (bf16[1024,2048]{1,0:T(8,128)(2,1)S(1)}, bf16[1024,2048]{1,0:T(8,128)(2,1)}, u32[]{:S(2)}) copy-start(bf16[1024,2048]{1,0:T(8,128)(2,1)} %add_convert_fusion) | copy-start | bytes 12582916
  481.4 12.7 %copy-start.26 = (bf16[1,1024,2048]{2,1,0:T(8,128)(2,1)S(1)}, bf16[1,1024,2048]{2,1,0:T(8,128)(2,1)}, u32[]{:S(2)}) copy-start(bf16[1,1024,2048]{2,1,0:T(8,128)(2,1)} %all-gather.11.cloned.1.call-done) | copy-start | bytes 12582916
  481.4 12.7 %copy-start.28 = (bf16[1024,8,64]{0,2,1:T(8,128)(2,1)S(1)}, bf16[1024,8,64]{0,2,1:T(8,128)(2,1)}, u32[]{:S(2)}) copy-start(bf16[1024,8,64]{0,2,1:T(8,128)(2,1)} %copy-done.27) | copy-start | bytes 3145732
  494.1 4.4 copy-start.7
  494.1 4.4 copy-start.24
  498.5 9.5 %copy-start.3 = (bf16[1,256,2048]{2,1,0:T(8,128)(2,1)S(1)}, bf16[1,256,2048]{2,1,0:T(8,128)(2,1)}, u32[]{:S(2)}) copy-start(bf16[1,256,2048]{2,1,0:T(8,128)(2,1)} %param.14) | copy-start | bytes 3145732
  498.5 9.5 %copy-start.9 = (f32[2048]{0:T(1024)S(1)}, f32[2048]{0:T(1024)}, u32[]{:S(2)}) copy-start(f32[2048]{0:T(1024)} %copy-done.8) | copy-start | bytes 24580
  498.5 9.5 %copy-start.15 = (f32[256]{0:T(256)S(1)}, f32[256]{0:T(256)}, u32[]{:S(2)}) copy-start(f32[256]{0:T(256)} %copy-done.14) | copy-start | bytes 3076
  498.5 9.5 %copy-start.17 = (f32[256]{0:T(256)S(1)}, f32[256]{0:T(256)}, u32[]{:S(2)}) copy-start(f32[256]{0:T(256)} %copy-done.16) | copy-start | bytes 3076
  498.6 11.8 %copy-start.10 = (f32[2048]{0:T(1024)S(1)}, f32[2048]{0:T(1024)}, u32[]{:S(2)}) copy-start(f32[2048]{0:T(1024)} %get-tuple-element.14) | copy-start | bytes 24580
  498.6 11.8 %copy-start.11 = (f32[2048]{0:T(1024)S(1)}, f32[2048]{0:T(1024)}, u32[]{:S(2)}) copy-start(f32[2048]{0:T(1024)} %get-tuple-element.20) | copy-start | bytes 24580
  498.6 11.8 %copy-start.12 = (f32[2048]{0:T(1024)S(1)}, f32[2048]{0:T(1024)}, u32[]{:S(2)}) copy-start(f32[2048]{0:T(1024)} %get-tuple-element.24) | copy-start | bytes 24580
  498.6 11.8 %copy-start.13 = (f32[2048]{0:T(1024)S(1)}, f32[2048]{0:T(1024)}, u32[]{:S(2)}) copy-start(f32[2048]{0:T(1024)} %get-tuple-element.28) | copy-start | bytes 24580
  498.6 26.8 %copy-start.1 = (bf16[8,64,2048]{2,1,0:T(8,128)(2,1)S(1)}, bf16[8,64,2048]{2,1,0:T(8,128)(2,1)}, u32[]{:S(2)}) copy-start(bf16[8,64,2048]{2,1,0:T(8,128)(2,1)} %param.20) | copy-start | bytes 6291460
  (7 other events, 5.3 us)
Sparse Core Ops, SparseCore 0:
  15.3 34.3 all-gather.4
  99.2 38.2 reduce-scatter.4
  141.7 31.5 all-gather.6
  174.7 31.4 all-gather.8
  239.9 38.2 reduce-scatter.8
  281.2 38.2 reduce-scatter.6
  325.1 31.4 all-gather.10
  465.9 38.2 reduce-scatter.10
where the time goes:
time: 542 us; the launch traced here: 533 us
  matrix products  255 us (47%)
  waiting for transfers between devices  215 us (40%)
  other arithmetic  28.6 us (5%)
  between operations  14.9 us (3%)
  blocking collectives  10.8 us (2%)
  local copies, waits for them, and re-layouts  7.72 us (1%)
    reduce_scatter x1, waiting for transfers between devices, device_step(): lax.psum_scatter(mlp_part, 'tp', scatter_dimension=1, tiled=True)  38.3 us
    reduce_scatter x1, waiting for transfers between devices, device_step(): lax.psum_scatter(attn_part, 'tp', scatter_dimension=1, tiled=True)  37.7 us
    all_gather x1, waiting for transfers between devices, device_step(): normed1_all = lax.all_gather(normed1, 'tp', axis=1, tiled=True)  34.1 us
    dot_general x1, matrix products, attention_backward(): jnp.einsum('bhqk,bqhe->bkhe', grad_scores, qkv_proj[0], preferred_element...  33.7 us
    dot_general x1, matrix products, attention_backward(): jnp.einsum('bhqk,bkhe->bqhe', grad_scores, qkv_proj[1], preferred_element...  33.4 us
    all_gather x1, waiting for transfers between devices, device_step(): grad_resid1_all = lax.all_gather(grad_resid1, 'tp', axis=1, tiled=True)  31.4 us
    all_gather x1, waiting for transfers between devices, device_step(): normed2_all = lax.all_gather(normed2, 'tp', axis=1, tiled=True)  31 us
    reduce_scatter x1, waiting for transfers between devices, device_step(): lax.psum_scatter(grad_norm2_part, 'tp', scatter_dimension=1, tiled=True)  22.2 us
  transfers between devices with their start and end apart: 8, of which 7 were waited for; matrix products, arithmetic and copies ran while one was open for 14% of the time, Pallas kernels for 0%

commit v1 on v0

v1 whole, which is shorter than its diff:
```python
import functools
import math

import jax
import jax.numpy as jnp
from jax import lax
from jax.experimental import pallas as pl
from jax.experimental.pallas import tpu as pltpu
from jax.sharding import PartitionSpec as P

LN_EPS = 1e-5
F32 = jnp.float32
BF16 = jnp.bfloat16
BLK = 256
NB = 4
GELU_C = math.sqrt(2.0 / math.pi)
GELU_A = 0.044715


def mm(a, b, ca, cb):
    return lax.dot_general(a, b, (((ca,), (cb,)), ((), ())), preferred_element_type=F32)


def sds(shape, dtype=BF16):
    return jax.ShapeDtypeStruct(shape, dtype)


def whole(shape):
    return pl.BlockSpec(shape, lambda *_: (0,) * len(shape))


def call(body, name, grid, ins, in_specs, outs, out_specs, flops=0, scratch=()):
    moved = sum(math.prod(a.shape) * a.dtype.itemsize for a in list(ins) + list(outs))
    return pl.pallas_call(
        body,
        grid=grid,
        in_specs=in_specs,
        out_specs=out_specs,
        out_shape=outs,
        scratch_shapes=list(scratch),
        compiler_params=pltpu.CompilerParams(vmem_limit_bytes=56 << 20),
        cost_estimate=pl.CostEstimate(flops=int(flops) + moved * 100, bytes_accessed=moved, transcendentals=0),
        name=name,
    )(*ins)


def causal_mask():
    rows = lax.broadcasted_iota(jnp.int32, (BLK, BLK), 0)
    cols = lax.broadcasted_iota(jnp.int32, (BLK, BLK), 1)
    return rows <= cols


def lanes(block):
    return pl.ds(pl.multiple_of(block * BLK, BLK), BLK)


def in_order(dst, near, far, index):
    me = lax.axis_index("tp")
    for j in range(NB):
        src = near if j < 2 else far
        dst[:, lanes(jnp.bitwise_xor(me, j))] = src[index + (slice(None), slice((j % 2) * BLK, (j % 2 + 1) * BLK))]


def out_of_order(src, near, far, index):
    me = lax.axis_index("tp")
    for j in range(NB):
        dst = near if j < 2 else far
        dst[index + (slice(None), slice((j % 2) * BLK, (j % 2 + 1) * BLK))] = src[:, lanes(jnp.bitwise_xor(me, j))]


def attn_fwd_kernel(scale, near_ref, far_ref, on_ref, of_ref, st_ref, q_s, k_s, v_s, o_s):
    for part, dst in enumerate((q_s, k_s, v_s)):
        in_order(dst, near_ref, far_ref, (part, 0))
    kt = k_s[...].T
    vt = v_s[...]
    mask = causal_mask()
    for c in range(NB):
        cols = slice(c * BLK, (c + 1) * BLK)
        n = (c + 1) * BLK
        q = q_s[:, cols]
        s = [mm(kt[i * BLK:(i + 1) * BLK], q, 1, 0) for i in range(c + 1)]
        s[c] = jnp.where(mask, s[c], -1e30)
        m = functools.reduce(jnp.maximum, [jnp.max(t, axis=0, keepdims=True) for t in s])
        e = [jnp.exp2((t - m) * scale) for t in s]
        r = 1.0 / functools.reduce(jnp.add, [jnp.sum(t, axis=0, keepdims=True) for t in e])
        p = jnp.concatenate([(t * r).astype(BF16) for t in e], axis=0)
        o_s[:, cols] = mm(vt[:, :n], p, 1, 0).astype(BF16)
        st_ref[0, 0:1, cols] = m
        st_ref[0, 1:2, cols] = r
    out_of_order(o_s, on_ref, of_ref, (0,))


def attn_bwd_kernel(scale, attn_scale, near_ref, far_ref, don_ref, dof_ref, st_ref, dn_ref, df_ref, q_s, k_s, v_s, do_s, d_s, p_ref, ds_ref):
    for part, dst in enumerate((q_s, k_s, v_s)):
        in_order(dst, near_ref, far_ref, (part, 0))
    in_order(do_s, don_ref, dof_ref, (0,))
    kt = k_s[...].T
    vt = v_s[...].T
    mask = causal_mask()
    for c in range(NB):
        cols = slice(c * BLK, (c + 1) * BLK)
        n = (c + 1) * BLK
        m = st_ref[0, 0:1, cols]
        r = st_ref[0, 1:2, cols]
        s = mm(kt[:n], q_s[:, cols], 1, 0)
        p = jnp.exp2((s - m) * scale) * r
        diag = jnp.where(mask, p[c * BLK:], 0.0)
        p = diag if c == 0 else jnp.concatenate([p[: c * BLK], diag], axis=0)
        p_ref[:n, cols] = p.astype(BF16)
        dp = mm(vt[:n], do_s[:, cols], 1, 0).astype(BF16).astype(F32)
        row_dot = jnp.sum(dp * p, axis=0, keepdims=True)
        ds = (p * (dp - row_dot)).astype(BF16)
        ds_ref[:n, cols] = ds
        d_s[0, :, cols] = (mm(k_s[:, :n], ds, 1, 0) * attn_scale).astype(BF16)
    for i in range(NB):
        rows = slice(i * BLK, (i + 1) * BLK)
        d_s[1, :, rows] = (mm(q_s[:, i * BLK:], ds_ref[rows, i * BLK:], 1, 1) * attn_scale).astype(BF16)
        d_s[2, :, rows] = mm(do_s[:, i * BLK:], p_ref[rows, i * BLK:], 1, 1).astype(BF16)
    for part in range(3):
        out_of_order(d_s.at[part], dn_ref, df_ref, (part, 0))


def attn_forward(near, far):
    _, heads, dim, half = near.shape
    attn_scale = dim ** -0.5
    qkv_spec = pl.BlockSpec((3, 1, dim, half), lambda h: (0, h, 0, 0))
    o_spec = pl.BlockSpec((1, dim, half), lambda h: (h, 0, 0))
    vm = pltpu.VMEM((dim, 2 * half), BF16)
    return call(
        functools.partial(attn_fwd_kernel, attn_scale * math.log2(math.e)), "attn_fwd", (heads,),
        [near, far], [qkv_spec, qkv_spec],
        [sds((heads, dim, half)), sds((heads, dim, half)), sds((heads, 2, 2 * half), F32)],
        [o_spec, o_spec, pl.BlockSpec((1, 2, 2 * half), lambda h: (h, 0, 0))],
        10e9, [vm] * 4)


def attn_backward(near, far, do_near, do_far, stats):
    _, heads, dim, half = near.shape
    attn_scale = dim ** -0.5
    qkv_spec = pl.BlockSpec((3, 1, dim, half), lambda h: (0, h, 0, 0))
    o_spec = pl.BlockSpec((1, dim, half), lambda h: (h, 0, 0))
    vm = pltpu.VMEM((dim, 2 * half), BF16)
    big = pltpu.VMEM((2 * half, 2 * half), BF16)
    return call(
        functools.partial(attn_bwd_kernel, attn_scale * math.log2(math.e), attn_scale), "attn_bwd", (heads,),
        [near, far, do_near, do_far, stats],
        [qkv_spec, qkv_spec, o_spec, o_spec, pl.BlockSpec((1, 2, 2 * half), lambda h: (h, 0, 0))],
        [sds(near.shape), sds(far.shape)], [qkv_spec, qkv_spec],
        22e9, [vm] * 4 + [pltpu.VMEM((3, dim, 2 * half), BF16), big, big])


def lay(dst, pieces):
    row = 0
    for piece in pieces:
        n = piece.shape[0]
        dst[row:row + n] = piece[...]
        row += n


def act_weight(pieces, w, name, transposed, out_rows=None, keep=False, step=512):
    rows = sum(p.shape[0] for p in pieces)
    inner = pieces[0].shape[1]
    n = w.shape[0] if transposed else w.shape[1]
    out_rows = out_rows or rows
    n_out = rows // out_rows
    n_in = len(pieces)

    def body(*refs):
        ins, w_ref, outs, a_ref = refs[:n_in], refs[n_in], refs[n_in + 1:n_in + 1 + n_out], refs[n_in + 1 + n_out]

        @pl.when(pl.program_id(0) == 0)
        def _():
            lay(a_ref, ins)

        t = mm(a_ref[...], w_ref[...], 1, 1 if transposed else 0).astype(BF16)
        for i, o in enumerate(outs):
            o[...] = t[i * out_rows:(i + 1) * out_rows]

    w_spec = pl.BlockSpec((step, inner), lambda i: (i, 0)) if transposed else pl.BlockSpec((inner, step), lambda i: (0, i))
    outs = [sds((out_rows, n))] * n_out
    out_specs = [pl.BlockSpec((out_rows, step), lambda i: (0, i))] * n_out
    scratch = [pltpu.VMEM((rows, inner), BF16)]
    if keep:
        outs, out_specs, scratch = outs + [sds((rows, inner))], out_specs + [whole((rows, inner))], []
    return call(body, name, (n // step,), list(pieces) + [w], [whole(p.shape) for p in pieces] + [w_spec], outs, out_specs, 2.0 * rows * inner * n, scratch)


def weight_act(w, pieces, name, bias=None, step=512):
    rows = sum(p.shape[0] for p in pieces)
    m, inner = w.shape
    n_in = len(pieces)
    has_bias = bias is not None

    def body(*refs):
        ins, w_ref = refs[:n_in], refs[n_in]
        o_ref, a_ref = refs[-2:]

        @pl.when(pl.program_id(0) == 0)
        def _():
            lay(a_ref, ins)

        t = mm(w_ref[...], a_ref[...], 1, 1)
        if has_bias:
            t = t + refs[n_in + 1][...]
        o_ref[...] = t.astype(BF16)

    ins = list(pieces) + [w] + ([bias] if has_bias else [])
    specs = [whole(p.shape) for p in pieces] + [pl.BlockSpec((step, inner), lambda i: (i, 0))]
    specs += [pl.BlockSpec((step, 1), lambda i: (i, 0))] if has_bias else []
    return call(body, name, (m // step,), ins, specs, [sds((m, rows)), sds((rows, inner))],
                [pl.BlockSpec((step, rows), lambda i: (i, 0)), whole((rows, inner))], 2.0 * rows * inner * m)


def feat_weight(a, w, name, out_rows, step=512):
    inner, rows = a.shape
    n = w.shape[1]
    n_out = rows // out_rows

    def body(a_ref, w_ref, *refs):
        outs, t_ref = refs[:n_out], refs[n_out]

        @pl.when(pl.program_id(0) == 0)
        def _():
            t_ref[...] = a_ref[...].T

        t = mm(t_ref[...], w_ref[...], 1, 0).astype(BF16)
        for i, o in enumerate(outs):
            o[...] = t[i * out_rows:(i + 1) * out_rows]

    return call(body, name, (n // step,), [a, w], [whole(a.shape), pl.BlockSpec((inner, step), lambda i: (0, i))],
                [sds((out_rows, n))] * n_out, [pl.BlockSpec((out_rows, step), lambda i: (0, i))] * n_out, 2.0 * rows * inner * n,
                [pltpu.VMEM((rows, inner), BF16)])


def feat_act(a, b, name, step):
    m, n = a[0].shape[0], b[0].shape[1]
    k = len(a)

    def body(*refs):
        total = mm(refs[0][...], refs[k][...], 1, 0)
        for i in range(1, k):
            total = total + mm(refs[i][...], refs[k + i][...], 1, 0)
        refs[-1][...] = total

    return call(body, name, (m // step,), list(a) + list(b), [pl.BlockSpec((step, t.shape[1]), lambda i: (i, 0)) for t in a] + [whole(t.shape) for t in b],
                [sds((m, n), F32)], [pl.BlockSpec((step, n), lambda i: (i, 0))], 2.0 * m * n * sum(t.shape[0] for t in b))[0]


def act_act(a, b, slices, name, step=256):
    m, n = a[0].shape[1], b[0].shape[1]
    ka, kb = len(a), len(b)

    def body(*refs):
        at = jnp.concatenate([refs[i][lo:hi] for i, lo, hi in slices], axis=0)
        total, row = None, 0
        for i in range(kb):
            r = refs[ka + i]
            t = mm(at[row:row + r.shape[0]], r[...], 0, 0)
            row += r.shape[0]
            total = t if total is None else total + t
        refs[-1][...] = total

    return call(body, name, (m // step,), list(a) + list(b), [pl.BlockSpec((t.shape[0], step), lambda i: (0, i)) for t in a] + [whole(t.shape) for t in b],
                [sds((m, n), F32)], [pl.BlockSpec((step, n), lambda i: (i, 0))], 2.0 * m * n * sum(t.shape[0] for t in b))[0]


def mlp(h2, dg, dg_blocks, w_up, b_up, name, out_rows, step=512, sub=256):
    rows = sum(p.shape[0] for p in h2)
    d, f = w_up.shape
    n_out = rows // out_rows
    n_in = len(h2)
    n_dg = len(dg_blocks)
    dg_rows = rows // n_dg

    def body(*refs):
        ins, dgs = refs[:n_in], refs[n_in:n_in + n_dg]
        w_ref, b_ref = refs[n_in + n_dg:n_in + n_dg + 2]
        outs = refs[n_in + n_dg + 2:]
        dh_refs, g_ref, dz_ref, db_ref, a_ref, acc_ref = outs[:n_out], outs[n_out], outs[n_out + 1], outs[n_out + 2], outs[n_out + 3], outs[n_out + 4]
        i = pl.program_id(0)

        @pl.when(i == 0)
        def _():
            lay(a_ref, ins)
            acc_ref[...] = jnp.zeros_like(acc_ref)

        for j in range(step // sub):
            cols = slice(j * sub, (j + 1) * sub)
            z = (mm(a_ref[...], w_ref[:, cols], 1, 0) + b_ref[:, cols].astype(F32)).astype(BF16).astype(F32)
            z2 = z * z
            t = jnp.tanh(z * (GELU_C + GELU_C * GELU_A * z2))
            cdf = 0.5 * (1.0 + t)
            slope = cdf + ((cdf * (1.0 - t)) * z) * (GELU_C + 3.0 * GELU_C * GELU_A * z2)
            g_ref[:, cols] = (z * cdf).astype(BF16)
            grad = jnp.concatenate([r[:, cols] for r in dgs], axis=0).astype(F32) if n_dg > 1 else dgs[0][:, cols].astype(F32)
            dz = (grad * slope).astype(BF16)
            dz_ref[:, cols] = dz
            db_ref[:, cols] = jnp.sum(dz.astype(F32), axis=0, keepdims=True)
        acc_ref[...] += mm(dz_ref[...], w_ref[...], 1, 1)

        @pl.when(i == pl.num_programs(0) - 1)
        def _():
            for k, o in enumerate(dh_refs):
                o[...] = acc_ref[k * out_rows:(k + 1) * out_rows].astype(BF16)

    def dg_spec(block):
        return pl.BlockSpec((dg_rows, step), lambda i: (block, i))

    ins = list(h2) + [dg] * n_dg + [w_up, b_up.reshape(1, f)]
    specs = [whole(p.shape) for p in h2] + [dg_spec(b) for b in dg_blocks] + [pl.BlockSpec((d, step), lambda i: (0, i)), pl.BlockSpec((1, step), lambda i: (0, i))]
    tile = pl.BlockSpec((rows, step), lambda i: (0, i))
    outs = [sds((out_rows, d))] * n_out + [sds((rows, f)), sds((rows, f)), sds((1, f), F32), sds((rows, d))]
    out_specs = [whole((out_rows, d))] * n_out + [tile, tile, pl.BlockSpec((1, step), lambda i: (0, i)), whole((rows, d))]
    res = call(body, name, (f // step,), ins, specs, outs, out_specs, 4.0 * rows * d * f, [pltpu.VMEM((rows, d), F32)])
    return list(res[:n_out]), res[n_out], res[n_out + 1], res[n_out + 2], res[n_out + 3]


def norm_stats(val32):
    centered = val32 - jnp.mean(val32, axis=-1, keepdims=True)
    inv_std = lax.rsqrt(jnp.mean(centered * centered, axis=-1, keepdims=True) + LN_EPS)
    return centered * inv_std, inv_std


def row_vec(v):
    return v.reshape(1, v.shape[0])


ROWS = 64


def row_spec(d, first=0):
    return pl.BlockSpec((ROWS, d), lambda i: (i + first, 0))


def norm_first(x, gain, shift, chunk, rows):
    d = x.shape[1]

    def body(x_ref, g_ref, s_ref, o_ref):
        x_hat, _ = norm_stats(x_ref[...].astype(F32))
        o_ref[...] = (x_hat * g_ref[...].astype(F32) + s_ref[...].astype(F32)).astype(BF16)

    return call(body, "norm1", (rows // ROWS,), [x, row_vec(gain), row_vec(shift)], [row_spec(d, chunk * rows // ROWS), whole((1, d)), whole((1, d))],
                [sds((rows, d))], [row_spec(d)])[0]


def norm_second(x, parts, bias, gain, shift, chunk, rows):
    d = x.shape[1]

    def body(x_ref, p0, p1, p2, b_ref, g_ref, s_ref, x1_ref, o_ref):
        total = p0[...].astype(F32) + p1[...].astype(F32) + p2[...].astype(F32)
        x1 = (x_ref[...].astype(F32) + total + b_ref[...].astype(F32)).astype(BF16)
        x1_ref[...] = x1
        x_hat, _ = norm_stats(x1.astype(F32))
        o_ref[...] = (x_hat * g_ref[...].astype(F32) + s_ref[...].astype(F32)).astype(BF16)

    vecs = [row_vec(bias), row_vec(gain), row_vec(shift)]
    return call(body, "norm2", (rows // ROWS,), [x] + parts + vecs, [row_spec(d, chunk * rows // ROWS)] + [row_spec(d)] * 3 + [whole((1, d))] * 3,
                [sds((rows, d))] * 2, [row_spec(d)] * 2)


def norm_back(parts, value, value_at, other, other_at, gain, rows, name):
    d = gain.shape[0]

    def body(p0, p1, p2, v_ref, y_ref, g_ref, o_ref, s_ref):
        grad = (p0[...].astype(F32) + p1[...].astype(F32) + p2[...].astype(F32)).astype(BF16).astype(F32)
        x_hat, inv_std = norm_stats(v_ref[...].astype(F32))
        scaled = grad * g_ref[...].astype(F32)
        back = inv_std * (scaled - jnp.mean(scaled, axis=-1, keepdims=True) - x_hat * jnp.mean(scaled * x_hat, axis=-1, keepdims=True))
        y = y_ref[...].astype(F32)
        out = (y + back).astype(BF16)
        o_ref[...] = out
        sums = [jnp.sum(t, axis=0, keepdims=True) for t in (grad * x_hat, grad, out.astype(F32), y)]
        first = pl.program_id(0) == 0
        for k, t in enumerate(sums):
            s_ref[k:k + 1] = jnp.where(first, t, s_ref[k:k + 1] + t)

    return call(body, name, (rows // ROWS,), parts + [value, other, row_vec(gain)],
                [row_spec(d)] * 3 + [row_spec(d, value_at * rows // ROWS), row_spec(d, other_at * rows // ROWS), whole((1, d))],
                [sds((rows, d)), sds((4, d), F32)], [row_spec(d), whole((4, d))])


def over_chip(value):
    return lax.ppermute(value, "tp", [(i, i ^ 1) for i in range(NB)])


def over_link(value):
    return lax.ppermute(value, "tp", [(i, i ^ 2) for i in range(NB)])


def after(value, *others):
    return lax.optimization_barrier((value,) + others)[0]


def add2(a, b):
    return (a.astype(F32) + b.astype(F32)).astype(BF16)


def sum_over_group(value):
    value = value + over_chip(value)
    return value + over_link(value)


def solution(mesh):
    def device_step(hidden, grad_out, ln1_gain, ln1_bias, w_qkv, b_qkv, w_out, b_out, ln2_gain, ln2_bias, w_up, b_up, w_down, b_down):
        d_model, _, heads, dim = w_qkv.shape
        x = hidden[0]
        dy_0 = grad_out[0]
        half = x.shape[0] // 2
        feats = heads * dim
        wt_qkv = jnp.transpose(w_qkv, (1, 2, 3, 0)).reshape(3 * feats, d_model)
        bias_qkv = b_qkv.astype(F32).reshape(3 * feats, 1)
        wo = w_out.reshape(feats, d_model)

        h1_0 = [norm_first(x, ln1_gain, ln1_bias, i, half) for i in range(2)]
        h1_2 = [over_link(t) for t in h1_0]
        h1_1 = [over_chip(t) for t in h1_0]
        dy_1 = over_chip(dy_0)
        dg_near, dy_near = act_weight([dy_0, dy_1], w_down, "dg", True, keep=True)
        qkv_near, h1_near = weight_act(wt_qkv, [h1_0[0], h1_0[1], after(h1_1[0], dg_near), h1_1[1]], "qkv", bias_qkv)
        h1_3 = [over_chip(t) for t in h1_2]
        dy_2 = over_link(after(dy_0, h1_2[0]))
        dy_3 = over_chip(dy_2)
        qkv_far, h1_far = weight_act(wt_qkv, [after(h1_2[0], qkv_near), h1_2[1], h1_3[0], h1_3[1]], "qkv", bias_qkv)
        shape = (3, heads, dim, 2 * BLK)
        qkv_near, qkv_far = qkv_near.reshape(shape), qkv_far.reshape(shape)
        ctx_near, ctx_far, stats = attn_forward(qkv_near, qkv_far)
        ctx_near, ctx_far = ctx_near.reshape(feats, 2 * BLK), ctx_far.reshape(feats, 2 * BLK)

        pf = feat_weight(ctx_far, wo, "out_proj", half)
        pn = feat_weight(after(ctx_near, pf[0]), wo, "out_proj", half)
        pf3 = [over_chip(t) for t in pf[2:]]
        pn1 = [over_chip(t) for t in pn[2:]]
        sent = [add2(pf[i], after(pf3[i], pn[0])) for i in range(2)]
        attn_x = [over_link(t) for t in sent]
        dg_far, dy_far = act_weight([after(dy_2, sent[1]), dy_3], w_down, "dg", True, keep=True)
        x1, h2_0, h2_1, h2_2, h2_3 = [], [], [], [], []
        for i in range(2):
            a, b = norm_second(x, [pn[i], pn1[i], after(attn_x[i], dg_far)], b_out, ln2_gain, ln2_bias, i, half)
            x1.append(a)
            h2_0.append(b)
            h2_2.append(over_link(b))
            h2_1.append(over_chip(b))
        h2_3 = [over_chip(t) for t in h2_2]

        dn, g_near, dz_near, db_near, h2_near = mlp([h2_0[0], h2_0[1], h2_1[0], h2_1[1]], dg_near, (0,), w_up, b_up, "mlp_near", half)
        dn1 = [over_chip(t) for t in dn[2:]]
        dfa, g_fa, dz_fa, db_fa, h2_fa = mlp([after(h2_2[0], dz_near), h2_3[0]], dg_far, (0, 2), w_up, b_up, "mlp_far", half)
        fa3 = over_chip(dfa[1])
        y_near = act_weight([after(g_near, dz_fa)], w_down, "y", False, half)
        sent_a = add2(dfa[0], after(fa3, y_near[0]))
        dh2_x = [over_link(sent_a)]
        dfb, g_fb, dz_fb, db_fb, h2_fb = mlp([after(h2_2[1], sent_a), h2_3[1]], dg_far, (1, 3), w_up, b_up, "mlp_far", half)
        fb3 = over_chip(dfb[1])
        y_far = act_weight([after(g_fa, dz_fb), g_fb], w_down, "y", False, half)
        sent_b = add2(dfb[0], after(fb3, y_far[0]))
        dh2_x.append(over_link(sent_b))
        grad_b_up = (db_near + db_fa + db_fb)[0]
        grad_w_down = act_act([after(g_near, sent_b), g_fa, g_fb], [dy_near, dy_far], [(0, 0, 512), (1, 0, 128), (2, 0, 128), (1, 128, 256), (2, 128, 256)], "dw_down")
        dx1_0, dx1_1, dx1_2, sums2 = [], [], [], []
        cover = [y_far[0], grad_w_down]
        for i in range(2):
            a, b = norm_back([dn[i], dn1[i], after(dh2_x[i], cover[i])], x1[i], 0, dy_0, i, ln2_gain, half, "norm2_back")
            dx1_0.append(a)
            sums2.append(b)
            dx1_2.append(over_link(a))
            dx1_1.append(over_chip(a))
        dx1_3 = [over_chip(t) for t in dx1_2]
        grad_w_up = act_act([after(h2_near, dx1_0[1]), h2_fa, h2_fb], [dz_near, dz_fa, dz_fb], [(0, 0, 512), (1, 0, 256), (2, 0, 256)], "dw_up")

        yf3 = [over_chip(y_far[1]), over_chip(y_far[3])]
        yn1 = [over_chip(t) for t in y_near[2:]]
        y_x = [over_link(add2(after(y_far[2 * i], dx1_2[0]), yf3[i])) for i in range(2)]

        do_near, dx1_near = weight_act(wo, [after(dx1_0[0], grad_w_up), dx1_0[1], dx1_1[0], dx1_1[1]], "d_ctx")
        do_far, dx1_far = weight_act(wo, [after(dx1_2[0], do_near), dx1_2[1], dx1_3[0], dx1_3[1]], "d_ctx")
        d_near, d_far = attn_backward(qkv_near, qkv_far, do_near.reshape(heads, dim, 2 * BLK), do_far.reshape(heads, dim, 2 * BLK), stats)
        d_near, d_far = d_near.reshape(3 * feats, 2 * BLK), d_far.reshape(3 * feats, 2 * BLK)
        hf = feat_weight(d_far, wt_qkv, "dh1", half)
        hf3 = [over_chip(t) for t in hf[2:]]
        hn = feat_weight(after(d_near, hf[0]), wt_qkv, "dh1", half)
        hn1 = [over_chip(t) for t in hn[2:]]
        sent = [add2(hf[i], after(hf3[i], hn[0])) for i in range(2)]
        dh1_x = [over_link(t) for t in sent]
        grad_wt_qkv = feat_act([after(d_near, sent[1]), d_far], [h1_near, h1_far], "dw_qkv", 256)
        grad_w_out = feat_act([after(ctx_near, grad_wt_qkv), ctx_far], [dx1_near, dx1_far], "dw_out", 256)
        grad_b_qkv = (jnp.sum(d_near, axis=1, dtype=F32) + jnp.sum(d_far, axis=1, dtype=F32)).reshape(3, heads, dim)
        y = []
        for i in range(2):
            total = yn1[i].astype(F32) + y_near[i].astype(F32) + after(y_x[i], grad_w_out).astype(F32)
            y.append((x1[i].astype(F32) + total + b_down.astype(F32)).astype(BF16))
        layer_out = jnp.concatenate(y, axis=0)
        early = sum_over_group(after(sums2[0] + sums2[1], sent[1]))
        dx, sums1 = [], []
        for i in range(2):
            a, b = norm_back([hn[i], hn1[i], after(dh1_x[i], grad_w_out)], x, i, dx1_0[i], 0, ln1_gain, half, "norm1_back")
            dx.append(a)
            sums1.append(b)
        grad_hidden = jnp.concatenate(dx, axis=0)
        late = sum_over_group((sums1[0] + sums1[1])[:2])
        grad_w_qkv = jnp.transpose(grad_wt_qkv.reshape(3, heads, dim, d_model), (3, 0, 1, 2))
        return (layer_out[None], grad_hidden[None], late[0], late[1], grad_w_qkv, grad_b_qkv, grad_w_out.reshape(heads, dim, d_model),
                early[2], early[0], early[1], grad_w_up, grad_b_up, grad_w_down, early[3])

    act_spec = P("dp", "tp", None)
    vec_spec = P(None)
    group_vec = P("dp")
    in_specs = (act_spec, act_spec, vec_spec, vec_spec, P(None, None, "tp", None), P(None, "tp", None), P("tp", None, None), vec_spec, vec_spec, vec_spec, P(None, "tp"), P("tp"), P("tp", None), vec_spec)
    out_specs = (act_spec, act_spec, group_vec, group_vec, P("dp", None, "tp", None), P("dp", "tp", None), P(("dp", "tp"), None, None), group_vec, group_vec, group_vec, P("dp", "tp"), P(("dp", "tp")), P(("dp", "tp"), None), group_vec)
    return jax.shard_map(device_step, mesh=mesh, in_specs=in_specs, out_specs=out_specs, check_vma=False)
```

time: 542 us -> 364 us (0.67); the launches traced: 533 us -> 362 us
  matrix products: 255 us -> 0 us
  Pallas kernels: 0 us -> 239 us
  waiting for transfers between devices: 215 us -> 62.9 us
  starting transfers between devices: 0.5 us -> 28.2 us
  other arithmetic: 28.6 us -> 8.28 us
  local copies, waits for them, and re-layouts: 7.72 us -> 22.1 us
  between operations: 14.9 us -> 1.33 us
  blocking collectives: 10.8 us -> 0 us
    pallas_call x0 -> x29, Pallas kernels: none -> 239 us  [call(): pl.pallas_call(body, grid=grid, in_specs=in_specs, out_specs=out_specs, o...]
    dot_general x15 -> x0, matrix products: 217 us -> none  [the longest x1 33.7 us: attention_backward(): jnp.einsum('bhqk,bqhe->bkhe', grad_scores, qkv_proj[0], preferred_element...]
    all_gather x4 -> x0, waiting for transfers between devices: 116 us -> none  [the longest x1 34.1 us: device_step(): normed1_all = lax.all_gather(normed1, 'tp', axis=1, tiled=True)]
    reduce_scatter x4 -> x0, waiting for transfers between devices: 98.3 us -> none  [the longest x1 38.3 us: device_step(): lax.psum_scatter(mlp_part, 'tp', scatter_dimension=1, tiled=True)]
    ppermute x0 -> x49, waiting for transfers between devices: none -> 62.9 us  [the longest x17 62.3 us: over_link(): return lax.ppermute(value, 'tp', [(i, i ^ 2) for i in range(NB)])]
    ppermute x0 -> x49, starting transfers between devices: none -> 28.2 us  [the longest x17 20.2 us: over_link(): return lax.ppermute(value, 'tp', [(i, i ^ 2) for i in range(NB)])]
    unnamed x2 -> x0, matrix products: 19.5 us -> none
    sub x1 -> x0, matrix products: 19.1 us -> none  [attention_forward(): probs32 = jax.nn.softmax(jnp.where(causal, scores, -1e+30), axis=-1)]
  transfers between devices with their start and end apart: 8 -> 49, of which waited for: 7 -> 8; matrix products, arithmetic and copies ran while one was open for 14% -> 4% of each run, Pallas kernels for 0% -> 65%
where the time goes in v1:
time: 364 us; the launch traced here: 362 us
  Pallas kernels  239 us (66%)
  waiting for transfers between devices  62.9 us (17%)
  starting transfers between devices  28.2 us (8%)
  local copies, waits for them, and re-layouts  22.1 us (6%)
  other arithmetic  8.28 us (2%)
    pallas_call x29, Pallas kernels, call(): pl.pallas_call(body, grid=grid, in_specs=in_specs, out_specs=out_specs, o...  239 us
    ppermute x17, waiting for transfers between devices, over_link(): return lax.ppermute(value, 'tp', [(i, i ^ 2) for i in range(NB)])  62.3 us
    ppermute x17, starting transfers between devices, over_link(): return lax.ppermute(value, 'tp', [(i, i ^ 2) for i in range(NB)])  20.2 us
    unnamed x130, local copies, waits for them, and re-layouts  14.2 us
    ppermute x32, starting transfers between devices, over_chip(): return lax.ppermute(value, 'tp', [(i, i ^ 1) for i in range(NB)])  8.06 us
  transfers between devices with their start and end apart: 49, of which 8 were waited for; matrix products, arithmetic and copies ran while one was open for 4% of the time, Pallas kernels for 65%

profile of v1, /device:TPU:0, one launch (start us, length us, event | category | flops | bytes accessed | tf_op | source)
XLA Modules:
  0.0 362.2 jit_solution(13626670709248732431)
XLA Ops:
  13.4 8.4 %collective-permute-done.3.refs_0_ = bf16[128,2048]{1,0:T(8,128)(2,1)S(1)} collective-permute-done((bf16[128,2048]{1,0:T(8,128)(2,1)}, bf16[128,2048]{1,0:T(8,128)(2,1)S(1)}, u32[]{:S(2)}, u32[]{:S(2)}) %collective-permute-start.3) | collective-permute-done | bytes 524320 | tf_op jit(solution)/shard_map/ppermute | solution.py:387
  23.8 9.2 %collective-permute-done.4.refs_1_ = bf16[128,2048]{1,0:T(8,128)(2,1)S(1)} collective-permute-done((bf16[128,2048]{1,0:T(8,128)(2,1)}, bf16[128,2048]{1,0:T(8,128)(2,1)S(1)}, u32[]{:S(2)}, u32[]{:S(2)}) %collective-permute-start.4) | collective-permute-done | bytes 524320 | tf_op jit(solution)/shard_map/ppermute | solution.py:387
  34.0 8.9 %dg.2 = (bf16[512,2048]{1,0:T(8,128)(2,1)}, bf16[512,2048]{1,0:T(8,128)(2,1)}) custom-call(bf16[256,2048]{1,0:T(8,128)(2,1)} %bitcast.36, bf16[256,2048]{1,0:T(8,128)(2,1)} %copy-done.42, bf16[2048,2048]{1,0:T(8,128)(2,1)} %refs_2_.5), custom_call_target="tpu_custom_call" | custom-call | flops 5762973696 | bytes 14680064 | tf_op jit(solution)/shard_map/dg/pallas_call | solution.py:34
  42.9 7.6 %qkv.2 = (bf16[1536,512]{1,0:T(8,128)(2,1)}, bf16[512,2048]{1,0:T(8,128)(2,1)}) custom-call(bf16[128,2048]{1,0:T(8,128)(2,1)} %norm1.2.refs_0_, bf16[128,2048]{1,0:T(8,128)(2,1)} %norm1.3.refs_1_, bf16[128,2048]{1,0:T(8,128)(2,1)} %collective-permute-done.refs_2_, bf16[128,2048]{1,0:T(8,128)(2,1)} %collective-permute-done.2.refs_3_, ...), custom_call_target="tpu_custom_call" | custom-call | flops 4427702272 | bytes 12064768 | tf_op jit(solution)/shard_map/qkv/pallas_call | solution.py:34
  52.0 7.5 %qkv.3 = (bf16[1536,512]{1,0:T(8,128)(2,1)}, bf16[512,2048]{1,0:T(8,128)(2,1)}) custom-call(bf16[128,2048]{1,0:T(8,128)(2,1)} %copy-done.53, bf16[128,2048]{1,0:T(8,128)(2,1)} %copy-done.54, bf16[128,2048]{1,0:T(8,128)(2,1)} %copy-done.60, bf16[128,2048]{1,0:T(8,128)(2,1)} %copy-done.62, bf16[1536,2048]{1,0:T(8,128)(2,1)} %bitcast.52, ...), custom_call_target="tpu_custom_call" | custom-call | flops 4427702272 | bytes 12064768 | tf_op jit(solution)/shard_map/qkv/pallas_call | solution.py:34
  59.6 17.1 %attn_fwd.1 = (bf16[8,64,512]{2,1,0:T(8,128)(2,1)}, bf16[8,64,512]{2,1,0:T(8,128)(2,1)}, f32[8,2,1024]{2,1,0:T(2,128)}) custom-call(bf16[3,8,64,512]{3,2,1,0:T(8,128)(2,1)} %bitcast.61, bf16[3,8,64,512]{3,2,1,0:T(8,128)(2,1)} %bitcast.63), custom_call_target="tpu_custom_call" | custom-call | flops 10425984000 | bytes 4259840 | tf_op jit(solution)/shard_map/attn_fwd/pallas_call | solution.py:34
  76.7 4.9 %out_proj.2 = (bf16[128,2048]{1,0:T(8,128)(2,1)}, bf16[128,2048]{1,0:T(8,128)(2,1)}, bf16[128,2048]{1,0:T(8,128)(2,1)}, bf16[128,2048]{1,0:T(8,128)(2,1)}) custom-call(bf16[512,512]{1,0:T(8,128)(2,1)} %bitcast.67, bf16[512,2048]{1,0:T(8,128)(2,1)} %bitcast.55), custom_call_target="tpu_custom_call" | custom-call | flops 1545601024 | bytes 4718592 | tf_op jit(solution)/shard_map/out_proj/pallas_call | solution.py:34
  84.4 5.0 %out_proj.3 = (bf16[128,2048]{1,0:T(8,128)(2,1)}, bf16[128,2048]{1,0:T(8,128)(2,1)}, bf16[128,2048]{1,0:T(8,128)(2,1)}, bf16[128,2048]{1,0:T(8,128)(2,1)}) custom-call(bf16[512,512]{1,0:T(8,128)(2,1)} %bitcast.65, bf16[512,2048]{1,0:T(8,128)(2,1)} %bitcast.56), custom_call_target="tpu_custom_call" | custom-call | flops 1545601024 | bytes 4718592 | tf_op jit(solution)/shard_map/out_proj/pallas_call | solution.py:34
  93.4 8.9 %dg.3 = (bf16[512,2048]{1,0:T(8,128)(2,1)}, bf16[512,2048]{1,0:T(8,128)(2,1)}) custom-call(bf16[256,2048]{1,0:T(8,128)(2,1)} %copy-done.41, bf16[256,2048]{1,0:T(8,128)(2,1)} %copy-done.43, bf16[2048,2048]{1,0:T(8,128)(2,1)} %refs_2_.5), custom_call_target="tpu_custom_call" | custom-call | flops 5762973696 | bytes 14680064 | tf_op jit(solution)/shard_map/dg/pallas_call | solution.py:34
  102.3 13.5 %collective-permute-done.9.p2 = bf16[128,2048]{1,0:T(8,128)(2,1)S(1)} collective-permute-done((bf16[128,2048]{1,0:T(8,128)(2,1)S(1)}, bf16[128,2048]{1,0:T(8,128)(2,1)S(1)}, u32[]{:S(2)}, u32[]{:S(2)}) %collective-permute-start.9) | collective-permute-done | bytes 524320 | tf_op jit(solution)/shard_map/ppermute | solution.py:387
  117.4 2.8 norm2.2
  122.9 2.8 norm2.3
  127.1 7.9 %collective-permute-done.17.refs_0_ = bf16[128,2048]{1,0:T(8,128)(2,1)S(1)} collective-permute-done((bf16[128,2048]{1,0:T(8,128)(2,1)}, bf16[128,2048]{1,0:T(8,128)(2,1)S(1)}, u32[]{:S(2)}, u32[]{:S(2)}) %collective-permute-start.17) | collective-permute-done | bytes 524320 | tf_op jit(solution)/shard_map/ppermute | solution.py:387
  136.6 18.2 %mlp_near.1 = (bf16[128,2048]{1,0:T(8,128)(2,1)}, bf16[128,2048]{1,0:T(8,128)(2,1)}, bf16[128,2048]{1,0:T(8,128)(2,1)}, bf16[128,2048]{1,0:T(8,128)(2,1)}, bf16[...) custom-call(bf16[128,2048]{1,0:T(8,128)(2,1)} %get-tuple-element.141.refs_0_, ...), custom_call_target="tpu_custom_call" | custom-call | flops 10688315392 | bytes 20983808 | tf_op jit(solution)/shard_map/mlp_near/pallas_call | solution.py:34
  155.7 10.9 %mlp_far.2 = (bf16[128,2048]{1,0:T(8,128)(2,1)}, bf16[128,2048]{1,0:T(8,128)(2,1)}, bf16[256,2048]{1,0:T(8,128)(2,1)}, bf16[256,2048]{1,0:T(8,128)(2,1)}, f32[1,2048]{1,0:T(1,128)}, /*index=5*/bf16[256,2048]{1,0:T(8,128)(2,1)}) custom-call(bf16[128,2048]{1,0:T(8,128)(2,1)} %copy-done.52, bf16[128,2048]{1,0:T(8,128)(2,1)} %copy-done.64, ...), custom_call_target="tpu_custom_call" | custom-call | flops 6078775296 | bytes 17838080 | tf_op jit(solution)/shard_map/mlp_far/pallas_call | solution.py:34
  167.7 8.8 %y.2 = (bf16[128,2048]{1,0:T(8,128)(2,1)}, bf16[128,2048]{1,0:T(8,128)(2,1)}, bf16[128,2048]{1,0:T(8,128)(2,1)}, bf16[128,2048]{1,0:T(8,128)(2,1)}) custom-call(bf16[512,2048]{1,0:T(8,128)(2,1)} %get-tuple-element.174.refs_0_, bf16[2048,2048]{1,0:T(8,128)(2,1)} %refs_2_.5), custom_call_target="tpu_custom_call" | custom-call | flops 5553258496 | bytes 12582912 | tf_op jit(solution)/shard_map/y/pallas_call | solution.py:34
  179.6 10.9 %mlp_far.3 = (bf16[128,2048]{1,0:T(8,128)(2,1)}, bf16[128,2048]{1,0:T(8,128)(2,1)}, bf16[256,2048]{1,0:T(8,128)(2,1)}, bf16[256,2048]{1,0:T(8,128)(2,1)}, f32[1,2048]{1,0:T(1,128)}, /*index=5*/bf16[256,2048]{1,0:T(8,128)(2,1)}) custom-call(bf16[128,2048]{1,0:T(8,128)(2,1)} %copy-done.49, bf16[128,2048]{1,0:T(8,128)(2,1)} %copy-done.61, ...), custom_call_target="tpu_custom_call" | custom-call | flops 6078775296 | bytes 17838080 | tf_op jit(solution)/shard_map/mlp_far/pallas_call | solution.py:34
  191.9 8.6 %y.3 = (bf16[128,2048]{1,0:T(8,128)(2,1)}, bf16[128,2048]{1,0:T(8,128)(2,1)}, bf16[128,2048]{1,0:T(8,128)(2,1)}, bf16[128,2048]{1,0:T(8,128)(2,1)}) custom-call(bf16[256,2048]{1,0:T(8,128)(2,1)} %get-tuple-element.159.refs_0_.refs_1_, bf16[256,2048]{1,0:T(8,128)(2,1)} %get-tuple-element.160.refs_1_.refs_2_, bf16[2048,2048]{1,0:T(8,128)(2,1)} %refs_2_.5), custom_call_target="tpu_custom_call" | custom-call | flops 5553258496 | bytes 12582912 | tf_op jit(solution)/shard_map/y/pallas_call | solution.py:34
  201.0 15.0 %dw_down.1 = f32[2048,2048]{1,0:T(8,128)} custom-call(bf16[512,2048]{1,0:T(8,128)(2,1)} %get-tuple-element.174.refs_0_, bf16[256,2048]{1,0:T(8,128)(2,1)} %get-tuple-element.159.refs_0_.refs_1_, bf16[256,2048]{1,0:T(8,128)(2,1)} %get-tuple-element.160.refs_1_.refs_2_, bf16[512,2048]{1,0:T(8,128)(2,1)} %get-tuple-element.175.refs_3_, ...), custom_call_target="tpu_custom_call" | custom-call | flops 11106516992 | bytes 25165824 | tf_op jit(solution)/shard_map/dw_down/pallas_call | solution.py:34
  217.1 3.8 %norm2_back.2 = (bf16[128,2048]{1,0:T(8,128)(2,1)}, f32[4,2048]{1,0:T(4,128)}) custom-call(bf16[128,2048]{1,0:T(8,128)(2,1)} %get-tuple-element.162.p0, bf16[128,2048]{1,0:T(8,128)(2,1)} %copy-done.22, bf16[128,2048]{1,0:T(8,128)(2,1)} %copy-done.26, bf16[128,2048]{1,0:T(8,128)(2,1)} %get-tuple-element.140.v_ref, bf16[256,2048]{1,0:T(8,128)(2,1)} %bitcast.37, ...), custom_call_target="tpu_custom_call" | custom-call | flops 370688000 | bytes 3706880 | tf_op jit(solution)/shard_map/norm2_back/pallas_call | solution.py:34
  223.5 3.6 %norm2_back.3 = (bf16[128,2048]{1,0:T(8,128)(2,1)}, f32[4,2048]{1,0:T(4,128)}) custom-call(bf16[128,2048]{1,0:T(8,128)(2,1)} %get-tuple-element.169.p0, bf16[128,2048]{1,0:T(8,128)(2,1)} %copy-done.21, bf16[128,2048]{1,0:T(8,128)(2,1)} %copy-done.28, bf16[128,2048]{1,0:T(8,128)(2,1)} %get-tuple-element.178.v_ref, bf16[256,2048]{1,0:T(8,128)(2,1)} %bitcast.38, ...), custom_call_target="tpu_custom_call" | custom-call | flops 370688000 | bytes 3706880 | tf_op jit(solution)/shard_map/norm2_back/pallas_call | solution.py:34
  227.5 15.3 %dw_up.1 = f32[2048,2048]{1,0:T(8,128)} custom-call(bf16[512,2048]{1,0:T(8,128)(2,1)} %get-tuple-element.180.refs_0_, bf16[256,2048]{1,0:T(8,128)(2,1)} %get-tuple-element.181.refs_1_, bf16[256,2048]{1,0:T(8,128)(2,1)} %get-tuple-element.182.refs_2_, bf16[512,2048]{1,0:T(8,128)(2,1)} %get-tuple-element.147.refs_3_, ...), custom_call_target="tpu_custom_call" | custom-call | flops 11106516992 | bytes 25165824 | tf_op jit(solution)/shard_map/dw_up/pallas_call | solution.py:34
  248.7 4.7 %d_ctx.2 = (bf16[512,512]{1,0:T(8,128)(2,1)}, bf16[512,2048]{1,0:T(8,128)(2,1)}) custom-call(bf16[128,2048]{1,0:T(8,128)(2,1)} %get-tuple-element.183.refs_0_.y_ref, bf16[128,2048]{1,0:T(8,128)(2,1)} %get-tuple-element.179.refs_1_.y_ref, bf16[128,2048]{1,0:T(8,128)(2,1)} %copy-done.55, bf16[128,2048]{1,0:T(8,128)(2,1)} %copy-done.57, bf16[512,2048]{1,0:T(8,128)(2,1)} %bitcast.57), custom_call_target="tpu_custom_call" | custom-call | flops 1755316224 | bytes 6815744 | tf_op jit(solution)/shard_map/d_ctx/pallas_call | solution.py:34
  255.1 4.7 %d_ctx.3 = (bf16[512,512]{1,0:T(8,128)(2,1)}, bf16[512,2048]{1,0:T(8,128)(2,1)}) custom-call(bf16[128,2048]{1,0:T(8,128)(2,1)} %copy-done.48, bf16[128,2048]{1,0:T(8,128)(2,1)} %copy-done.51, bf16[128,2048]{1,0:T(8,128)(2,1)} %copy-done.58, bf16[128,2048]{1,0:T(8,128)(2,1)} %copy-done.59, bf16[512,2048]{1,0:T(8,128)(2,1)} %bitcast.58), custom_call_target="tpu_custom_call" | custom-call | flops 1755316224 | bytes 6815744 | tf_op jit(solution)/shard_map/d_ctx/pallas_call | solution.py:34
  259.8 23.5 %attn_bwd.1 = (bf16[3,8,64,512]{3,2,1,0:T(8,128)(2,1)}, bf16[3,8,64,512]{3,2,1,0:T(8,128)(2,1)}) custom-call(bf16[3,8,64,512]{3,2,1,0:T(8,128)(2,1)} %bitcast.62, bf16[3,8,64,512]{3,2,1,0:T(8,128)(2,1)} %bitcast.64, bf16[8,64,512]{2,1,0:T(8,128)(2,1)} %bitcast.69, bf16[8,64,512]{2,1,0:T(8,128)(2,1)} %bitcast.70, f32[8,2,1024]{2,1,0:T(2,128)} %get-tuple-element.187.st_ref), custom_call_target="tpu_custom_call" | custom-call | flops 22740557824 | bytes 7405568 | tf_op jit(solution)/shard_map/attn_bwd/pallas_call | solution.py:34
  283.3 7.9 %dh1.2 = (bf16[128,2048]{1,0:T(8,128)(2,1)}, bf16[128,2048]{1,0:T(8,128)(2,1)}, bf16[128,2048]{1,0:T(8,128)(2,1)}, bf16[128,2048]{1,0:T(8,128)(2,1)}) custom-call(bf16[1536,512]{1,0:T(8,128)(2,1)} %bitcast.42, bf16[1536,2048]{1,0:T(8,128)(2,1)} %bitcast.53), custom_call_target="tpu_custom_call" | custom-call | flops 4217372672 | bytes 9961472 | tf_op jit(solution)/shard_map/dh1/pallas_call | solution.py:34
  292.3 7.7 %dh1.3 = (bf16[128,2048]{1,0:T(8,128)(2,1)}, bf16[128,2048]{1,0:T(8,128)(2,1)}, bf16[128,2048]{1,0:T(8,128)(2,1)}, bf16[128,2048]{1,0:T(8,128)(2,1)}) custom-call(bf16[1536,512]{1,0:T(8,128)(2,1)} %bitcast.40, bf16[1536,2048]{1,0:T(8,128)(2,1)} %bitcast.54), custom_call_target="tpu_custom_call" | custom-call | flops 4217372672 | bytes 9961472 | tf_op jit(solution)/shard_map/dh1/pallas_call | solution.py:34
  300.7 11.7 %dw_qkv.1 = f32[1536,2048]{1,0:T(8,128)} custom-call(bf16[1536,512]{1,0:T(8,128)(2,1)} %bitcast.41, bf16[1536,512]{1,0:T(8,128)(2,1)} %bitcast.43, bf16[512,2048]{1,0:T(8,128)(2,1)} %get-tuple-element.197.refs_2_, bf16[512,2048]{1,0:T(8,128)(2,1)} %get-tuple-element.198.refs_3_), custom_call_target="tpu_custom_call" | custom-call | flops 8434745344 | bytes 19922944 | tf_op jit(solution)/shard_map/dw_qkv/pallas_call | solution.py:34
  312.5 6.4 %dw_out.1 = f32[512,2048]{1,0:T(8,128)} custom-call(bf16[512,512]{1,0:T(8,128)(2,1)} %bitcast.66, bf16[512,512]{1,0:T(8,128)(2,1)} %bitcast.68, bf16[512,2048]{1,0:T(8,128)(2,1)} %get-tuple-element.200.refs_2_, bf16[512,2048]{1,0:T(8,128)(2,1)} %get-tuple-element.201.refs_3_), custom_call_target="tpu_custom_call" | custom-call | flops 3091202048 | bytes 9437184 | tf_op jit(solution)/shard_map/dw_out/pallas_call | solution.py:34
  324.8 20.4 %collective-permute-done.48 = f32[4,2048]{1,0:T(4,128)S(1)} collective-permute-done((f32[4,2048]{1,0:T(4,128)S(1)}, f32[4,2048]{1,0:T(4,128)S(1)}, u32[]{:S(2)}, u32[]{:S(2)}) %collective-permute-start.48) | collective-permute-done | bytes 32800 | tf_op jit(solution)/shard_map/ppermute | solution.py:387
  347.6 3.7 %norm1_back.2 = (bf16[128,2048]{1,0:T(8,128)(2,1)}, f32[4,2048]{1,0:T(4,128)}) custom-call(bf16[128,2048]{1,0:T(8,128)(2,1)} %get-tuple-element.194.p0, bf16[128,2048]{1,0:T(8,128)(2,1)} %copy-done.24, bf16[128,2048]{1,0:T(8,128)(2,1)} %copy-done.27, bf16[256,2048]{1,0:T(8,128)(2,1)} %bitcast.33, bf16[128,2048]{1,0:T(8,128)(2,1)} %get-tuple-element.183.refs_0_.y_ref, ...), custom_call_target="tpu_custom_call" | custom-call | flops 370688000 | bytes 3706880 | tf_op jit(solution)/shard_map/norm1_back/pallas_call | solution.py:34
  352.1 3.7 %norm1_back.3 = (bf16[128,2048]{1,0:T(8,128)(2,1)}, f32[4,2048]{1,0:T(4,128)}) custom-call(bf16[128,2048]{1,0:T(8,128)(2,1)} %get-tuple-element.214.p0, bf16[128,2048]{1,0:T(8,128)(2,1)} %copy-done.23, bf16[128,2048]{1,0:T(8,128)(2,1)} %copy-done.25, bf16[256,2048]{1,0:T(8,128)(2,1)} %bitcast.34, bf16[128,2048]{1,0:T(8,128)(2,1)} %get-tuple-element.179.refs_1_.y_ref, ...), custom_call_target="tpu_custom_call" | custom-call | flops 370688000 | bytes 3706880 | tf_op jit(solution)/shard_map/norm1_back/pallas_call | solution.py:34
  (255 shorter events, 66.7 us)
Async XLA Ops:
  0.7 32.3 %collective-permute-start.1 = (bf16[256,2048]{1,0:T(8,128)(2,1)}, bf16[256,2048]{1,0:T(8,128)(2,1)S(1)}, u32[]{:S(2)}, u32[]{:S(2)}) collective-permute-start(bf16[256,2048]{1,0:T(8,128)(2,1)} %bitcast.35), channel_id=1, source_target_pairs={{0,1},{1,0},{2,3},{3,2},{4,5},{5,4},{6,7},{7,6}} | collective-permute-start | bytes 3145736 | tf_op jit(solution)/shard_map/ppermute | solution.py:383
  6.4 15.4 %collective-permute-start.3 = (bf16[128,2048]{1,0:T(8,128)(2,1)}, bf16[128,2048]{1,0:T(8,128)(2,1)S(1)}, u32[]{:S(2)}, u32[]{:S(2)}) collective-permute-start(bf16[128,2048]{1,0:T(8,128)(2,1)} %norm1.2.refs_0_), channel_id=1, source_target_pairs={{0,2},{1,3},{2,0},{3,1},{4,6},{5,7},{6,4},{7,5}} | collective-permute-start | bytes 1572872 | tf_op jit(solution)/shard_map/ppermute | solution.py:387
  11.2 21.7 %collective-permute-start.4 = (bf16[128,2048]{1,0:T(8,128)(2,1)}, bf16[128,2048]{1,0:T(8,128)(2,1)S(1)}, u32[]{:S(2)}, u32[]{:S(2)}) collective-permute-start(bf16[128,2048]{1,0:T(8,128)(2,1)} %norm1.3.refs_1_), channel_id=1, source_target_pairs={{0,2},{1,3},{2,0},{3,1},{4,6},{5,7},{6,4},{7,5}} | collective-permute-start | bytes 1572872 | tf_op jit(solution)/shard_map/ppermute | solution.py:387
  11.2 31.6 %collective-permute-start = (bf16[128,2048]{1,0:T(8,128)(2,1)}, bf16[128,2048]{1,0:T(8,128)(2,1)}, u32[]{:S(2)}, u32[]{:S(2)}) collective-permute-start(bf16[128,2048]{1,0:T(8,128)(2,1)} %norm1.2.refs_0_), channel_id=1, source_target_pairs={{0,1},{1,0},{2,3},{3,2},{4,5},{5,4},{6,7},{7,6}} | collective-permute-start | bytes 1572872 | tf_op jit(solution)/shard_map/ppermute | solution.py:383
  11.4 31.5 %collective-permute-start.2 = (bf16[128,2048]{1,0:T(8,128)(2,1)}, bf16[128,2048]{1,0:T(8,128)(2,1)}, u32[]{:S(2)}, u32[]{:S(2)}) collective-permute-start(bf16[128,2048]{1,0:T(8,128)(2,1)} %norm1.3.refs_1_), channel_id=1, source_target_pairs={{0,1},{1,0},{2,3},{3,2},{4,5},{5,4},{6,7},{7,6}} | collective-permute-start | bytes 1572872 | tf_op jit(solution)/shard_map/ppermute | solution.py:383
  21.7 62.2 %collective-permute-start.10 = (bf16[256,2048]{1,0:T(8,128)(2,1)S(1)}, bf16[256,2048]{1,0:T(8,128)(2,1)S(1)}, u32[]{:S(2)}, u32[]{:S(2)}) collective-permute-start(bf16[256,2048]{1,0:T(8,128)(2,1)S(1)} %bitcast.39), channel_id=1, source_target_pairs={{0,2},{1,3},{2,0},{3,1},{4,6},{5,7},{6,4},{7,5}} | collective-permute-start | bytes 3145736 | tf_op jit(solution)/shard_map/ppermute | solution.py:387
  33.0 17.5 %collective-permute-start.5 = (bf16[128,2048]{1,0:T(8,128)(2,1)S(1)}, bf16[128,2048]{1,0:T(8,128)(2,1)S(1)}, u32[]{:S(2)}, u32[]{:S(2)}) collective-permute-start(bf16[128,2048]{1,0:T(8,128)(2,1)S(1)} %collective-permute-done.3.refs_0_), channel_id=1, source_target_pairs={{0,1},{1,0},{2,3},{3,2},{4,5},{5,4},{6,7},{7,6}} | collective-permute-start | bytes 1572872 | tf_op jit(solution)/shard_map/ppermute | solution.py:383
  33.0 17.5 %collective-permute-start.6 = (bf16[128,2048]{1,0:T(8,128)(2,1)S(1)}, bf16[128,2048]{1,0:T(8,128)(2,1)S(1)}, u32[]{:S(2)}, u32[]{:S(2)}) collective-permute-start(bf16[128,2048]{1,0:T(8,128)(2,1)S(1)} %collective-permute-done.4.refs_1_), channel_id=1, source_target_pairs={{0,1},{1,0},{2,3},{3,2},{4,5},{5,4},{6,7},{7,6}} | collective-permute-start | bytes 1572872 | tf_op jit(solution)/shard_map/ppermute | solution.py:383
  89.5 26.3 %collective-permute-start.7 = (bf16[128,2048]{1,0:T(8,128)(2,1)}, bf16[128,2048]{1,0:T(8,128)(2,1)S(1)}, u32[]{:S(2)}, u32[]{:S(2)}) collective-permute-start(bf16[128,2048]{1,0:T(8,128)(2,1)} %get-tuple-element.130), channel_id=1, source_target_pairs={{0,1},{1,0},{2,3},{3,2},{4,5},{5,4},{6,7},{7,6}} | collective-permute-start | bytes 1572872 | tf_op jit(solution)/shard_map/ppermute | solution.py:383
  89.7 32.3 %collective-permute-start.13 = (bf16[128,2048]{1,0:T(8,128)(2,1)}, bf16[128,2048]{1,0:T(8,128)(2,1)S(1)}, u32[]{:S(2)}, u32[]{:S(2)}) collective-permute-start(bf16[128,2048]{1,0:T(8,128)(2,1)} %get-tuple-element.143), channel_id=1, source_target_pairs={{0,1},{1,0},{2,3},{3,2},{4,5},{5,4},{6,7},{7,6}} | collective-permute-start | bytes 1572872 | tf_op jit(solution)/shard_map/ppermute | solution.py:383
  90.1 31.8 %collective-permute-start.14 = (bf16[128,2048]{1,0:T(8,128)(2,1)S(1)}, bf16[128,2048]{1,0:T(8,128)(2,1)S(1)}, u32[]{:S(2)}, u32[]{:S(2)}) collective-permute-start(bf16[128,2048]{1,0:T(8,128)(2,1)S(1)} %add_convert_fusion.8), channel_id=1, source_target_pairs={{0,2},{1,3},{2,0},{3,1},{4,6},{5,7},{6,4},{7,5}} | collective-permute-start | bytes 1572872 | tf_op jit(solution)/shard_map/ppermute | solution.py:387
  92.4 23.4 %collective-permute-start.9 = (bf16[128,2048]{1,0:T(8,128)(2,1)S(1)}, bf16[128,2048]{1,0:T(8,128)(2,1)S(1)}, u32[]{:S(2)}, u32[]{:S(2)}) collective-permute-start(bf16[128,2048]{1,0:T(8,128)(2,1)S(1)} %add_convert_fusion.9), channel_id=1, source_target_pairs={{0,2},{1,3},{2,0},{3,1},{4,6},{5,7},{6,4},{7,5}} | collective-permute-start | bytes 1572872 | tf_op jit(solution)/shard_map/ppermute | solution.py:387
  126.8 40.8 %collective-permute-start.20 = (bf16[128,2048]{1,0:T(8,128)(2,1)}, bf16[128,2048]{1,0:T(8,128)(2,1)S(1)}, u32[]{:S(2)}, u32[]{:S(2)}) collective-permute-start(bf16[128,2048]{1,0:T(8,128)(2,1)} %get-tuple-element.145.refs_1_), channel_id=1, source_target_pairs={{0,2},{1,3},{2,0},{3,1},{4,6},{5,7},{6,4},{7,5}} | collective-permute-start | bytes 1572872 | tf_op jit(solution)/shard_map/ppermute | solution.py:387
  135.0 19.9 %collective-permute-start.18 = (bf16[128,2048]{1,0:T(8,128)(2,1)S(1)}, bf16[128,2048]{1,0:T(8,128)(2,1)S(1)}, u32[]{:S(2)}, u32[]{:S(2)}) collective-permute-start(bf16[128,2048]{1,0:T(8,128)(2,1)S(1)} %collective-permute-done.17.refs_0_), channel_id=1, source_target_pairs={{0,1},{1,0},{2,3},{3,2},{4,5},{5,4},{6,7},{7,6}} | collective-permute-start | bytes 1572872 | tf_op jit(solution)/shard_map/ppermute | solution.py:383
  167.1 49.3 %collective-permute-start.23 = (bf16[128,2048]{1,0:T(8,128)(2,1)S(1)}, bf16[128,2048]{1,0:T(8,128)(2,1)S(1)}, u32[]{:S(2)}, u32[]{:S(2)}) collective-permute-start(bf16[128,2048]{1,0:T(8,128)(2,1)S(1)} %copy-done.46), channel_id=1, source_target_pairs={{0,1},{1,0},{2,3},{3,2},{4,5},{5,4},{6,7},{7,6}} | collective-permute-start | bytes 1572872 | tf_op jit(solution)/shard_map/ppermute | solution.py:383
  167.2 55.5 %collective-permute-start.28 = (bf16[128,2048]{1,0:T(8,128)(2,1)S(1)}, bf16[128,2048]{1,0:T(8,128)(2,1)S(1)}, u32[]{:S(2)}, u32[]{:S(2)}) collective-permute-start(bf16[128,2048]{1,0:T(8,128)(2,1)S(1)} %copy-done.44), channel_id=1, source_target_pairs={{0,1},{1,0},{2,3},{3,2},{4,5},{5,4},{6,7},{7,6}} | collective-permute-start | bytes 1572872 | tf_op jit(solution)/shard_map/ppermute | solution.py:383
  176.5 144.3 %collective-permute-start.19 = (bf16[128,2048]{1,0:T(8,128)(2,1)}, bf16[128,2048]{1,0:T(8,128)(2,1)S(1)}, u32[]{:S(2)}, u32[]{:S(2)}) collective-permute-start(bf16[128,2048]{1,0:T(8,128)(2,1)} %get-tuple-element.151), channel_id=1, source_target_pairs={{0,1},{1,0},{2,3},{3,2},{4,5},{5,4},{6,7},{7,6}} | collective-permute-start | bytes 1572872 | tf_op jit(solution)/shard_map/ppermute | solution.py:383
  177.0 39.1 %collective-permute-start.24 = (bf16[128,2048]{1,0:T(8,128)(2,1)S(1)}, bf16[128,2048]{1,0:T(8,128)(2,1)S(1)}, u32[]{:S(2)}, u32[]{:S(2)}) collective-permute-start(bf16[128,2048]{1,0:T(8,128)(2,1)S(1)} %add_convert_fusion.7), channel_id=1, source_target_pairs={{0,2},{1,3},{2,0},{3,1},{4,6},{5,7},{6,4},{7,5}} | collective-permute-start | bytes 1572872 | tf_op jit(solution)/shard_map/ppermute | solution.py:387
  200.7 20.2 %collective-permute-start.30 = (bf16[128,2048]{1,0:T(8,128)(2,1)S(1)}, bf16[128,2048]{1,0:T(8,128)(2,1)S(1)}, u32[]{:S(2)}, u32[]{:S(2)}) collective-permute-start(bf16[128,2048]{1,0:T(8,128)(2,1)S(1)} %add_convert_fusion.5), channel_id=1, source_target_pairs={{0,2},{1,3},{2,0},{3,1},{4,6},{5,7},{6,4},{7,5}} | collective-permute-start | bytes 1572872 | tf_op jit(solution)/shard_map/ppermute | solution.py:387
  216.1 26.7 %collective-permute-start.26 = (bf16[128,2048]{1,0:T(8,128)(2,1)S(1)}, bf16[128,2048]{1,0:T(8,128)(2,1)S(1)}, u32[]{:S(2)}, u32[]{:S(2)}) collective-permute-start(bf16[128,2048]{1,0:T(8,128)(2,1)S(1)} %copy-done.50), channel_id=1, source_target_pairs={{0,1},{1,0},{2,3},{3,2},{4,5},{5,4},{6,7},{7,6}} | collective-permute-start | bytes 1572872 | tf_op jit(solution)/shard_map/ppermute | solution.py:383
  216.3 27.1 %collective-permute-start.38 = (bf16[128,2048]{1,0:T(8,128)(2,1)S(1)}, bf16[128,2048]{1,0:T(8,128)(2,1)S(1)}, u32[]{:S(2)}, u32[]{:S(2)}) collective-permute-start(bf16[128,2048]{1,0:T(8,128)(2,1)S(1)} %copy-done.47), channel_id=1, source_target_pairs={{0,1},{1,0},{2,3},{3,2},{4,5},{5,4},{6,7},{7,6}} | collective-permute-start | bytes 1572872 | tf_op jit(solution)/shard_map/ppermute | solution.py:383
  220.9 21.8 %collective-permute-start.25 = (bf16[128,2048]{1,0:T(8,128)(2,1)}, bf16[128,2048]{1,0:T(8,128)(2,1)S(1)}, u32[]{:S(2)}, u32[]{:S(2)}) collective-permute-start(bf16[128,2048]{1,0:T(8,128)(2,1)} %get-tuple-element.183.refs_0_.y_ref), channel_id=1, source_target_pairs={{0,2},{1,3},{2,0},{3,1},{4,6},{5,7},{6,4},{7,5}} | collective-permute-start | bytes 1572872 | tf_op jit(solution)/shard_map/ppermute | solution.py:387
  227.1 19.2 %collective-permute-start.33 = (bf16[128,2048]{1,0:T(8,128)(2,1)}, bf16[128,2048]{1,0:T(8,128)(2,1)S(1)}, u32[]{:S(2)}, u32[]{:S(2)}) collective-permute-start(bf16[128,2048]{1,0:T(8,128)(2,1)} %get-tuple-element.179.refs_1_.y_ref), channel_id=1, source_target_pairs={{0,2},{1,3},{2,0},{3,1},{4,6},{5,7},{6,4},{7,5}} | collective-permute-start | bytes 1572872 | tf_op jit(solution)/shard_map/ppermute | solution.py:387
  246.5 74.4 %collective-permute-start.37 = (bf16[128,2048]{1,0:T(8,128)(2,1)}, bf16[128,2048]{1,0:T(8,128)(2,1)S(1)}, u32[]{:S(2)}, u32[]{:S(2)}) collective-permute-start(bf16[128,2048]{1,0:T(8,128)(2,1)} %get-tuple-element.203), channel_id=1, source_target_pairs={{0,1},{1,0},{2,3},{3,2},{4,5},{5,4},{6,7},{7,6}} | collective-permute-start | bytes 1572872 | tf_op jit(solution)/shard_map/ppermute | solution.py:383
  247.0 72.4 %collective-permute-start.27 = (bf16[128,2048]{1,0:T(8,128)(2,1)S(1)}, bf16[128,2048]{1,0:T(8,128)(2,1)S(1)}, u32[]{:S(2)}, u32[]{:S(2)}) collective-permute-start(bf16[128,2048]{1,0:T(8,128)(2,1)S(1)} %add_convert_fusion.6), channel_id=1, source_target_pairs={{0,2},{1,3},{2,0},{3,1},{4,6},{5,7},{6,4},{7,5}} | collective-permute-start | bytes 1572872 | tf_op jit(solution)/shard_map/ppermute | solution.py:387
  253.5 65.4 %collective-permute-start.39 = (bf16[128,2048]{1,0:T(8,128)(2,1)S(1)}, bf16[128,2048]{1,0:T(8,128)(2,1)S(1)}, u32[]{:S(2)}, u32[]{:S(2)}) collective-permute-start(bf16[128,2048]{1,0:T(8,128)(2,1)S(1)} %add_convert_fusion.2), channel_id=1, source_target_pairs={{0,2},{1,3},{2,0},{3,1},{4,6},{5,7},{6,4},{7,5}} | collective-permute-start | bytes 1572872 | tf_op jit(solution)/shard_map/ppermute | solution.py:387
  300.1 18.8 %collective-permute-start.41 = (bf16[128,2048]{1,0:T(8,128)(2,1)}, bf16[128,2048]{1,0:T(8,128)(2,1)S(1)}, u32[]{:S(2)}, u32[]{:S(2)}) collective-permute-start(bf16[128,2048]{1,0:T(8,128)(2,1)} %get-tuple-element.210), channel_id=1, source_target_pairs={{0,1},{1,0},{2,3},{3,2},{4,5},{5,4},{6,7},{7,6}} | collective-permute-start | bytes 1572872 | tf_op jit(solution)/shard_map/ppermute | solution.py:383
  318.9 27.2 %collective-permute-start.40 = (bf16[128,2048]{1,0:T(8,128)(2,1)}, bf16[128,2048]{1,0:T(8,128)(2,1)S(1)}, u32[]{:S(2)}, u32[]{:S(2)}) collective-permute-start(bf16[128,2048]{1,0:T(8,128)(2,1)} %get-tuple-element.209), channel_id=1, source_target_pairs={{0,1},{1,0},{2,3},{3,2},{4,5},{5,4},{6,7},{7,6}} | collective-permute-start | bytes 1572872 | tf_op jit(solution)/shard_map/ppermute | solution.py:383
  318.9 32.4 %collective-permute-start.43 = (bf16[128,2048]{1,0:T(8,128)(2,1)S(1)}, bf16[128,2048]{1,0:T(8,128)(2,1)S(1)}, u32[]{:S(2)}, u32[]{:S(2)}) collective-permute-start(bf16[128,2048]{1,0:T(8,128)(2,1)S(1)} %copy-done.45), channel_id=1, source_target_pairs={{0,1},{1,0},{2,3},{3,2},{4,5},{5,4},{6,7},{7,6}} | collective-permute-start | bytes 1572872 | tf_op jit(solution)/shard_map/ppermute | solution.py:383
  319.4 25.8 %collective-permute-start.44 = (bf16[128,2048]{1,0:T(8,128)(2,1)S(1)}, bf16[128,2048]{1,0:T(8,128)(2,1)S(1)}, u32[]{:S(2)}, u32[]{:S(2)}) collective-permute-start(bf16[128,2048]{1,0:T(8,128)(2,1)S(1)} %add_convert_fusion.4), channel_id=1, source_target_pairs={{0,2},{1,3},{2,0},{3,1},{4,6},{5,7},{6,4},{7,5}} | collective-permute-start | bytes 1572872 | tf_op jit(solution)/shard_map/ppermute | solution.py:387
  320.9 24.3 %collective-permute-start.42 = (bf16[128,2048]{1,0:T(8,128)(2,1)S(1)}, bf16[128,2048]{1,0:T(8,128)(2,1)S(1)}, u32[]{:S(2)}, u32[]{:S(2)}) collective-permute-start(bf16[128,2048]{1,0:T(8,128)(2,1)S(1)} %add_convert_fusion), channel_id=1, source_target_pairs={{0,2},{1,3},{2,0},{3,1},{4,6},{5,7},{6,4},{7,5}} | collective-permute-start | bytes 1572872 | tf_op jit(solution)/shard_map/ppermute | solution.py:387
  322.4 22.8 %collective-permute-start.48 = (f32[4,2048]{1,0:T(4,128)S(1)}, f32[4,2048]{1,0:T(4,128)S(1)}, u32[]{:S(2)}, u32[]{:S(2)}) collective-permute-start(f32[4,2048]{1,0:T(4,128)S(1)} %add.106), channel_id=1, source_target_pairs={{0,2},{1,3},{2,0},{3,1},{4,6},{5,7},{6,4},{7,5}} | collective-permute-start | bytes 98312 | tf_op jit(solution)/shard_map/ppermute | solution.py:387
  (82 other events, 613.6 us)
